TPU v7x, 32 devices: a whole 2x2x4 slice. The times are simulated.
32 devices in a mesh: sector: 8 (over y, x, core), block: 4 (over z).
Axes of the slice: x: 2, y: 2, z: 4, core: 2. Of those that a mesh axis runs over, the one named last changes fastest.
Arguments:
- source: float32 [125, 2, 128, 512], P(None, None, 'sector', 'block'), may hold values from -6 to 6
- jacobian: float32 [2, 128, 512], P(None, 'sector', 'block'), may hold values from 0.5 to 2
- stiff_fine: float32 [125, 125], replicated, may hold values from -1 to 2, as said below
- stiff_coarse: float32 [27, 27], replicated, may hold values from -1 to 2, as said below
- restrict_fine: float32 [27, 125], replicated, may hold values from -0.5 to 0.5
- restrict_coarse: float32 [8, 27], replicated, may hold values from -1.25 to 1.25
- mortar_proj: float32 [2, 5, 5], replicated, may hold values from -2.5 to 2.5
- rotor_trace: float32 [4, 25, 128, 512], P(None, None, 'sector', 'block'), may hold values from -6 to 6
- stator_trace: float32 [4, 25, 128, 512], P(None, None, 'sector', 'block'), may hold values from -6 to 6
- offsets: int32 [4], P('block'), may hold values from 0 to 127
Outputs:
- stator_flux: float32 [4, 25, 128, 512], P(None, None, 'sector', 'block')
- rotor_flux: float32 [4, 25, 128, 512], P(None, None, 'sector', 'block')
- fine_pressure: float32 [125, 2, 128, 512], P(None, None, 'sector', 'block')
- coarse_pressure: float32 [27, 2, 128, 512], P(None, None, 'sector', 'block')
- coarsest_residual: float32 [8, 2, 128, 512], P(None, None, 'sector', 'block')
Inputs may be any that keep to these rules, and one draw needn't show every extreme that they name: `stiff_fine`: symmetric, positive diagonal. `stiff_coarse`: symmetric, positive diagonal.
All inputs are finite; a program needn't handle non-finite values.
Results may differ from a plain program's by a relative error of at most 0.00016.
Values sent between devices are 32-bit elements; how exact they have to be, the bound alone decides.
No kernel may reach another device: no remote copies, remote signals or barrier semaphores. Data moves between devices by JAX's collectives and lax.ppermute only.
A program may use at most 128 MiB of HBM per device.

v0:
```python
import jax
import jax.numpy as jnp
from jax import lax
from jax.experimental import pallas as pl
from jax.experimental.pallas import tpu as pltpu
from jax.sharding import PartitionSpec as P


F32 = jnp.float32
BF16 = jnp.bfloat16
DAMPING = 0.6
PENALTY = 0.5
LANES = 128
NF = 5
NC = 3
LAST = 8
STEP = 2
HALO_UNROLL = 32
GROUP = {NF: 4, NC: 16}
GROUP_UNROLL = {NF: 4, NC: 1}
VMEM_BYTES = 12 * 1024 * 1024


def up(value, unit):
    return (value + unit - 1) // unit * unit


def any_spec():
    return pl.BlockSpec(memory_space=pl.ANY)


def hbm_spec():
    return pl.BlockSpec(memory_space=pltpu.HBM)


def in_vmem(array):
    return pltpu.with_memory_space_constraint(array, pltpu.VMEM)


def in_hbm(*arrays):
    return tuple(pltpu.with_memory_space_constraint(x, pltpu.HBM) for x in arrays)


def params(**extra):
    return pltpu.CompilerParams(vmem_limit_bytes=VMEM_BYTES, **extra)


def cost(flops, data):
    return pl.CostEstimate(flops=flops, bytes_accessed=data, transcendentals=0)


def parts_of(x):
    high = x.astype(BF16)
    low = (x - high.astype(F32)).astype(BF16)
    return high, low


def stacked(matrix):
    high, low = parts_of(matrix)
    top = jnp.concatenate([high, high], axis=1)
    bottom = jnp.concatenate([low, jnp.zeros_like(low)], axis=1)
    return jnp.concatenate([top, bottom], axis=0)


def times(weights, x):
    rows = weights.shape[0] // 2
    high, low = parts_of(x)
    both = jnp.dot(weights, jnp.concatenate([high, low], axis=0), preferred_element_type=F32)
    return both[:rows] + both[rows:]


def lane_ids(rows):
    return lax.broadcasted_iota(jnp.int32, (rows, LANES), 1)


def node_rows(shape, axis):
    return lax.broadcasted_iota(jnp.int32, shape, axis)


def digit(index, unit, most):
    found = jnp.zeros_like(index)
    for k in range(1, most + 1):
        found += jnp.where(index >= k * unit, 1, 0)
    return found


def half_faces(n, height):
    row = node_rows((height, LANES), 0)
    a = digit(row, n * n, n)
    b = digit(row - n * n * a, n, n - 1)
    on_a = jnp.where((a == 0) | (a == n - 1), PENALTY, 0.0)
    on_b = jnp.where((b == 0) | (b == n - 1), PENALTY, 0.0)
    return jnp.where(row < n**3, on_a + on_b, 0.0)


def turn_plan(offset, span):
    total = span * lax.axis_size("sector")
    flipped = jnp.where(offset >= total // 2, 1, 0)
    return flipped, jnp.where(flipped == 1, total - 1 - offset, offset)


def smem_spec():
    return pl.BlockSpec(memory_space=pltpu.SMEM)


def add_halo(n, e_total, span, source_of, r_ref, c1, c2, z1, z2):
    nn = n * n
    odd = lax.rem(lax.axis_index("sector"), 2) == 1
    block = lax.axis_index("block")
    z_odd = lax.rem(block, 2) == 1
    lowest = block == 0
    highest = block == lax.axis_size("block") - 1
    lanes = lane_ids(8)

    def slab(e, carry):
        r_ref[e] = source_of(e)
        for a in range(n):
            first, second = z1[a], z2[a]
            below = jnp.where(z_odd, first, second)
            above = jnp.where(z_odd, second, first)
            below = pltpu.roll(below, lax.rem(LANES - e, LANES), 1)
            above = pltpu.roll(above, LANES - 1 - e, 1)
            below = jnp.where((lanes == 0) & jnp.logical_not(lowest), PENALTY * below, 0.0)
            above = jnp.where((lanes == LANES - 1) & jnp.logical_not(highest), PENALTY * above, 0.0)
            r_ref[e, pl.ds(a * nn, n), :] += below[:n]
            r_ref[e, pl.ds(a * nn + nn - n, n), :] += above[:n]
        return carry

    lax.fori_loop(0, e_total, slab, 0, unroll=HALO_UNROLL)
    for layer in range(e_total // span):
        first, second = c1[layer], c2[layer]
        r_ref[layer * span, pl.ds(0, nn), :] += PENALTY * jnp.where(odd, first, second)
        r_ref[layer * span + span - 1, pl.ds((n - 1) * nn, nn), :] += PENALTY * jnp.where(odd, second, first)


def correct(n, e_total, span, r_ref, u_ref, u_of, c1, c2, z1, z2):
    nn = n * n
    lanes = lane_ids(8)

    def slab(e, carry):
        lows, highs = carry
        u_ref[e] = u_of(e, r_ref[e])
        new_lows, new_highs = [], []
        for a in range(n):
            low = u_ref[e, pl.ds(a * nn, 8), :]
            high = u_ref[e, pl.ds(a * nn + nn - n, 8), :]
            here = lanes == e
            new_lows.append(jnp.where(here, pltpu.roll(low, e, 1), lows[a]))
            new_highs.append(jnp.where(here, pltpu.roll(high, e + 1, 1), highs[a]))
        return tuple(new_lows), tuple(new_highs)

    blank = tuple(jnp.zeros((8, LANES), F32) for _ in range(n))
    lows, highs = lax.fori_loop(0, e_total, slab, (blank, blank), unroll=HALO_UNROLL)
    odd = lax.rem(lax.axis_index("sector"), 2) == 1
    z_odd = lax.rem(lax.axis_index("block"), 2) == 1
    for a in range(n):
        z1[a] = jnp.where(z_odd, lows[a], highs[a])
        z2[a] = jnp.where(z_odd, highs[a], lows[a])
    for layer in range(e_total // span):
        low = u_ref[layer * span, pl.ds(0, nn), :]
        high = u_ref[layer * span + span - 1, pl.ds((n - 1) * nn, nn), :]
        c1[layer] = jnp.where(odd, low, high)
        c2[layer] = jnp.where(odd, high, low)


def subtract_operator(n, e_total, span, r_ref, u_ref, weights, jac_ref, count_ref):
    nn = n * n
    group = GROUP[n]
    lanes = lane_ids(8)

    def some(i, carry):
        first = i * group
        wide = jnp.concatenate([u_ref[first + j] for j in range(group)], axis=1)
        product = times(weights[...], wide)
        for j in range(group):
            e = first + j
            own = product[:, j * LANES : (j + 1) * LANES]
            r_ref[e] = r_ref[e] - jac_ref[pl.ds(e, 1), :] * own - count_ref[...] * u_ref[e]
            s = lax.rem(e, span)
            before = jnp.where(s > 0, PENALTY, 0.0)
            after = jnp.where(s < span - 1, PENALTY, 0.0)
            previous = u_ref[jnp.maximum(e - 1, 0), pl.ds((n - 1) * nn, nn), :]
            following = u_ref[jnp.minimum(e + 1, e_total - 1), pl.ds(0, nn), :]
            r_ref[e, pl.ds(0, nn), :] += before * previous
            r_ref[e, pl.ds((n - 1) * nn, nn), :] += after * following
            for a in range(n):
                low = u_ref[e, pl.ds(a * nn, 8), :]
                high = u_ref[e, pl.ds(a * nn + nn - n, 8), :]
                from_below = jnp.where(lanes > 0, PENALTY * pltpu.roll(high, 1, 1), 0.0)
                from_above = jnp.where(lanes < LANES - 1, PENALTY * pltpu.roll(low, LANES - 1, 1), 0.0)
                r_ref[e, pl.ds(a * nn, n), :] += from_below[:n]
                r_ref[e, pl.ds(a * nn + nn - n, n), :] += from_above[:n]
        return carry

    lax.fori_loop(0, e_total // group, some, 0, unroll=GROUP_UNROLL[n])


def face_shapes(n, layers):
    circ = jax.ShapeDtypeStruct((layers, n * n, LANES), F32)
    axial = jax.ShapeDtypeStruct((n, 8, LANES), F32)
    return [circ, circ, axial, axial]


def prepare(offsets, rotor, stator, mortar, stiff_fine, stiff_coarse, restrict_fine, restrict_coarse):
    rows, span = rotor.shape[0], rotor.shape[1]
    tall, wide = up(rows, 8), up(rows, 16)
    big, small = up(NF**3, 16), up(NC**3, 16)
    smalls = (mortar, stiff_fine, stiff_coarse, restrict_fine, restrict_coarse)

    def body(
        offset_ref, rotor_ref, stator_ref, mortar_in, kf_in, kc_in, rf_in, rc_in,
        pair_out, near1_out, near2_out, proj_out, back_out, wf_out, wc_out, rfs_out, rcs_out, df_out, dc_out,
        mortar_ref, kf_ref, kc_ref, rf_ref, rc_ref, pad_ref, sem, small_sem,
    ):
        flipped, _ = turn_plan(offset_ref[0], span)
        copies = []
        for f in range(span):
            for source, first in ((rotor_ref, span * flipped), (stator_ref, span - span * flipped)):
                if tall > rows:
                    pair_out[first + f, pl.ds(rows, tall - rows), :] = jnp.zeros((tall - rows, LANES), F32)
                copies.append(
                    pltpu.make_async_copy(source.at[:, f, :], pair_out.at[first + f, pl.ds(0, rows), :], sem)
                )
        little = [
            pltpu.make_async_copy(source, target, small_sem)
            for source, target in (
                (mortar_in, mortar_ref), (kf_in, kf_ref), (kc_in, kc_ref), (rf_in, rf_ref), (rc_in, rc_ref)
            )
        ]
        for c in little + copies:
            c.start()
        row, col = node_rows((tall, LANES), 0), node_rows((tall, LANES), 1)
        comp_r, comp_c = digit(row, NF * NF, 4), digit(col, NF * NF, 5)
        rest_r, rest_c = row - NF * NF * comp_r, col - NF * NF * comp_c
        a_r, a_c = digit(rest_r, NF, NF - 1), digit(rest_c, NF, NF - 1)
        same = (comp_r == comp_c) & (rest_r - NF * a_r == rest_c - NF * a_c) & (row < rows) & (col < rows)
        ahead = jnp.where(same, a_r * NF + a_c, -1)
        turned = jnp.where(same, a_c * NF + a_r, -1)
        for c in little:
            c.wait()

        def both_terms(pair):
            highs, lows = zip(*[parts_of(m) for m in pair])
            return jnp.concatenate(
                [jnp.concatenate([h, h], axis=1) for h in highs]
                + [jnp.concatenate([l, jnp.zeros_like(l)], axis=1) for l in lows],
                axis=0,
            )

        for found, out in ((ahead, proj_out), (turned, back_out)):
            pair = []
            for which in range(2):
                total = jnp.zeros((tall, LANES), F32)
                matrix = mortar_ref[:, which, :]
                for i in range(NF):
                    for j in range(NF):
                        total = jnp.where(found == i * NF + j, matrix[i : i + 1, j : j + 1], total)
                pair.append(total)
            out[...] = both_terms([m[:, :wide] for m in pair])

        def padded(ref, height, width):
            pad_ref[...] = jnp.zeros_like(pad_ref)
            pad_ref[pl.ds(0, ref.shape[0]), pl.ds(0, ref.shape[1])] = ref[...]
            return pad_ref[pl.ds(0, height), :][:, :width]

        for ref, out, diag_out, size in ((kf_ref, wf_out, df_out, big), (kc_ref, wc_out, dc_out, small)):
            matrix = padded(ref, size, size)
            out[...] = stacked(matrix)
            row = lax.broadcasted_iota(jnp.int32, (size, size), 0)
            col = lax.broadcasted_iota(jnp.int32, (size, size), 1)
            diag = jnp.sum(jnp.where(row == col, matrix, 0.0), axis=1, keepdims=True)
            diag = jnp.where(row[:, :1] < ref.shape[0], diag, 1.0)
            diag_out[...] = jnp.broadcast_to(diag, (size, LANES))
        rfs_out[...] = stacked(padded(rf_ref, small, big))
        rcs_out[...] = stacked(padded(rc_ref, 16, small))
        for c in copies:
            c.wait()
        odd = lax.rem(lax.axis_index("sector"), 2) == 1
        lowest, highest = pair_out[span * flipped], pair_out[span * flipped + span - 1]
        near1_out[0] = jnp.where(odd, lowest, highest)
        near2_out[0] = jnp.where(odd, highest, lowest)

    return pl.pallas_call(
        body,
        out_shape=[
            jax.ShapeDtypeStruct((2 * span, tall, LANES), F32),
            jax.ShapeDtypeStruct((1, tall, LANES), F32),
            jax.ShapeDtypeStruct((1, tall, LANES), F32),
            jax.ShapeDtypeStruct((4 * tall, 2 * wide), BF16),
            jax.ShapeDtypeStruct((4 * tall, 2 * wide), BF16),
            jax.ShapeDtypeStruct((2 * big, 2 * big), BF16),
            jax.ShapeDtypeStruct((2 * small, 2 * small), BF16),
            jax.ShapeDtypeStruct((2 * small, 2 * big), BF16),
            jax.ShapeDtypeStruct((32, 2 * small), BF16),
            jax.ShapeDtypeStruct((big, LANES), F32),
            jax.ShapeDtypeStruct((small, LANES), F32),
        ],
        in_specs=[smem_spec()] + [hbm_spec()] * 7,
        scratch_shapes=[pltpu.VMEM(m.shape, F32) for m in smalls]
        + [pltpu.VMEM((big, LANES), F32), pltpu.SemaphoreType.DMA, pltpu.SemaphoreType.DMA],
        compiler_params=params(),
        name="prepare",
    )(offsets, *in_hbm(rotor, stator, *smalls))


def apply_faces(matrix_ref, slab_of, count, tall, wide, y0, y1, unrolled):
    group = 4
    fill = jnp.zeros((wide - tall, group * LANES), F32)

    def some(i, carry):
        first = group * i
        least = min if unrolled else jnp.minimum
        x = jnp.concatenate([slab_of(least(first + j, count - 1)) for j in range(group)], axis=1)
        if wide > tall:
            x = jnp.concatenate([x, fill], axis=0)
        high, low = parts_of(x)
        y = jnp.dot(matrix_ref[...], jnp.concatenate([high, low], axis=0), preferred_element_type=F32)
        a = y[:tall] + y[2 * tall : 3 * tall]
        b = y[tall : 2 * tall] + y[3 * tall :]
        for j in range(group):
            y0[first + j] = a[:, j * LANES : (j + 1) * LANES]
            y1[first + j] = b[:, j * LANES : (j + 1) * LANES]
        return carry

    if unrolled:
        for i in range(up(count, group) // group):
            some(i, 0)
    else:
        lax.fori_loop(0, up(count, group) // group, some, 0)


def own_part(offsets, pair, proj, jac, diag):
    span, tall = pair.shape[0] // 2, pair.shape[1]
    wide = proj.shape[1] // 2
    e_total, height = jac.shape[0], diag.shape[0]

    def body(offset_ref, pair_ref, proj_ref, jac_ref, diag_ref, kept, w_ref, y0, y1):
        first = span * turn_plan(offset_ref[0], span)[0]
        apply_faces(proj_ref, lambda f: pair_ref[first + f], span, tall, wide, y0, y1, False)
        kept[0] = y0[0]
        kept[span] = y1[span - 1]

        def face(g, carry):
            kept[g] = y0[g] + y1[g - 1]
            return carry

        lax.fori_loop(1, span, face, 0)
        count = half_faces(NF, height)

        def weight(e, carry):
            w_ref[e] = DAMPING / (jac_ref[pl.ds(e, 1), :] * diag_ref[...] + count)
            return carry

        lax.fori_loop(0, e_total, weight, 0)

    return pl.pallas_call(
        body,
        out_shape=[
            jax.ShapeDtypeStruct((span + 1, tall, LANES), F32),
            jax.ShapeDtypeStruct((e_total, height, LANES), F32),
        ],
        in_specs=[smem_spec()] + [pl.BlockSpec()] * 4,
        scratch_shapes=[pltpu.VMEM((up(span, 4), tall, LANES), F32)] * 2,
        compiler_params=params(),
        cost_estimate=cost(2 * 10**9, 10 * 10**6),
        name="own_part",
    )(offsets, pair, proj, jac, diag)


def copy_faces(source, first, out, into, count):
    def one(f, carry):
        out[into + f] = source[first + f]
        return carry

    lax.fori_loop(0, count, one, 0)


def cut(pair, many, few):
    span = pair.shape[0] // 2

    def body(pair_ref, far, near, near_back, far_back):
        copy_faces(pair_ref, span - few, far, 0, few)
        copy_faces(pair_ref, 0, near, 0, many)
        copy_faces(pair_ref, 2 * span - many, near_back, 0, many)
        copy_faces(pair_ref, span, far_back, 0, few)

    piece = [pltpu.VMEM((count,) + pair.shape[1:], F32) for count in (few, many, many, few)]
    return pl.pallas_call(body, out_shape=piece, compiler_params=params(), name="cut")(pair)


def join(far, near, near_back, far_back):
    few, many = far.shape[0], near.shape[0]
    reach = few + many

    def body(far_ref, near_ref, near_back_ref, far_back_ref, out, sem):
        first = 0
        copies = []
        for piece in (far_ref, near_ref, near_back_ref, far_back_ref):
            count = piece.shape[0]
            copies.append(pltpu.make_async_copy(piece, out.at[pl.ds(first, count)], sem))
            first += count
        for c in copies:
            c.start()
        for c in copies:
            c.wait()

    return pl.pallas_call(
        body,
        out_shape=jax.ShapeDtypeStruct((2 * reach,) + far.shape[1:], F32),
        out_specs=hbm_spec(),
        scratch_shapes=[pltpu.SemaphoreType.DMA],
        compiler_params=params(),
        name="join",
    )(far, near, near_back, far_back)


def first_sweep(offsets, wins, pair, kept, near1, near2, proj, back, source, w, jac, weights, layers):
    span, tall = pair.shape[0] // 2, pair.shape[1]
    reach = wins.shape[0] // 2
    wide = back.shape[1] // 2
    rows = 4 * NF * NF
    e_total = jac.shape[0]
    n, nn = NF, NF * NF
    nodes = n**3
    height = weights.shape[0] // 2

    def body(
        offset_ref, wins_in, pair_ref, kept_ref, near1_ref, near2_ref, proj_ref, back_ref, source_ref, w_ref,
        jac_ref, w_mat, sflux_out, rflux_out, r_ref, u_ref, c1, c2, z1, z2,
        y0, y1, x0, x1, sflux, rflux, count_ref, wins_ref, in_sem, out_sem, win_sems,
    ):
        loads = [
            pltpu.make_async_copy(source_ref.at[:, e, :], r_ref.at[e, pl.ds(0, nodes), :], in_sem)
            for e in range(e_total)
        ]
        flipped, steps = turn_plan(offset_ref[0], span)
        inner = lax.rem(steps, STEP)
        rotor_half = reach * flipped
        halves = [
            pltpu.make_async_copy(wins_in.at[pl.ds(first, reach)], wins_ref.at[pl.ds(first, reach)], win_sems.at[k])
            for k, first in enumerate((rotor_half, reach - rotor_half))
        ]
        for c in halves + loads:
            c.start()
        ahead, behind = STEP - 1 - inner, reach + inner
        first_rotor = jnp.where(flipped == 1, behind, ahead)
        first_stator = jnp.where(flipped == 1, ahead, behind)
        own_stator = span - span * flipped
        count_ref[...] = half_faces(n, height)
        odd = lax.rem(lax.axis_index("sector"), 2) == 1

        def rotor_slab(f):
            if f <= span:
                return wins_ref[first_rotor + f]
            one, two = near1_ref[0], near2_ref[0]
            return jnp.where(odd, one, two) if f == span + 1 else jnp.where(odd, two, one)

        def jump(f):
            own = kept_ref[f]
            if f == 0:
                own = own + x1[span + 1]
            if f == span:
                own = own + x0[span + 2]
            return wins_ref[first_stator + f] - own

        halves[0].wait()
        apply_faces(proj_ref, rotor_slab, span + 3, tall, wide, x0, x1, True)
        halves[1].wait()
        apply_faces(back_ref, jump, span + 1, tall, wide, y0, y1, True)
        stores = []
        for s in range(span):
            sflux[s] = pair_ref[own_stator + s] - (x0[s + 1] + x1[s])
            rflux[s] = y0[s] + y1[s + 1]
            for buffer, out in ((sflux, sflux_out), (rflux, rflux_out)):
                c = pltpu.make_async_copy(buffer.at[s, pl.ds(0, rows), :], out.at[:, s, :], out_sem)
                c.start()
                stores.append(c)
        for c in loads:
            c.wait()
        for s in range(span):
            if height > nodes:
                for layer in range(layers):
                    r_ref[layer * span + s, pl.ds(nodes, height - nodes), :] = jnp.zeros((height - nodes, LANES), F32)
            inflow = sflux[s, pl.ds(0, nn), :] + sflux[s, pl.ds(3 * nn, nn), :]
            outflow = rflux[s, pl.ds(0, nn), :] + rflux[s, pl.ds(3 * nn, nn), :]
            r_ref[span + s, pl.ds(0, nn, stride=n), :] += inflow
            r_ref[s, pl.ds(n - 1, nn, stride=n), :] += -outflow
        correct(n, e_total, span, r_ref, u_ref, lambda e, r: r * w_ref[e], c1, c2, z1, z2)
        subtract_operator(n, e_total, span, r_ref, u_ref, w_mat, jac_ref, count_ref)
        for c in stores:
            c.wait()

    whole = pl.BlockSpec()
    field = jax.ShapeDtypeStruct((e_total, height, LANES), F32)
    trace = jax.ShapeDtypeStruct((rows, span, LANES), F32)
    slabs = pltpu.VMEM((up(span + 3, 4), tall, LANES), F32)
    return pl.pallas_call(
        body,
        out_shape=[trace, trace, field, field] + face_shapes(n, layers),
        in_specs=[smem_spec(), hbm_spec()] + [whole] * 6 + [hbm_spec()] + [whole] * 3,
        out_specs=[hbm_spec()] * 2 + [whole] * 6,
        scratch_shapes=[slabs] * 4
        + [
            pltpu.VMEM((span, tall, LANES), F32),
            pltpu.VMEM((span, tall, LANES), F32),
            pltpu.VMEM((height, LANES), F32),
            pltpu.VMEM(wins.shape, F32),
            pltpu.SemaphoreType.DMA,
            pltpu.SemaphoreType.DMA,
            pltpu.SemaphoreType.DMA((2,)),
        ],
        compiler_params=params(),
        cost_estimate=cost(2 * 10**9, 20 * 10**6),
        name="first_sweep",
    )(offsets, *in_hbm(wins), pair, kept, near1, near2, proj, back, *in_hbm(source), in_vmem(w), jac, weights)


def sweep(n, r, p, w, jac, weights, faces, layers, last):
    e_total, height = r.shape[0], r.shape[1]
    span = e_total // layers
    nodes = n**3

    def body(r_in, p_in, w_in, jac_ref, w_mat, h1, h2, g1, g2, p_out, r_ref, c1, c2, z1, z2, u_ref, p_keep, count_ref, sem):
        count_ref[...] = half_faces(n, height)
        p_ref = p_keep if last else p_out
        add_halo(n, e_total, span, lambda e: r_in[e], r_ref, h1, h2, g1, g2)

        def u_of(e, r_here):
            u = r_here * w_in[e]
            p_ref[e] = p_in[e] + u
            return u

        correct(n, e_total, span, r_ref, u_ref, u_of, c1, c2, z1, z2)
        stores = []
        if last:
            for e in range(e_total):
                c = pltpu.make_async_copy(p_ref.at[e, pl.ds(0, nodes), :], p_out.at[:, e, :], sem)
                c.start()
                stores.append(c)
        subtract_operator(n, e_total, span, r_ref, u_ref, w_mat, jac_ref, count_ref)
        for c in stores:
            c.wait()

    whole = pl.BlockSpec()
    field = jax.ShapeDtypeStruct((e_total, height, LANES), F32)
    kept = jax.ShapeDtypeStruct((nodes, e_total, LANES), F32) if last else field
    return pl.pallas_call(
        body,
        out_shape=[kept, field] + face_shapes(n, layers),
        out_specs=[any_spec() if last else whole] + [whole] * 5,
        scratch_shapes=[
            pltpu.VMEM((e_total, height, LANES), F32),
            pltpu.VMEM((e_total, height, LANES) if last else (1, 8, LANES), F32),
            pltpu.VMEM((height, LANES), F32),
            pltpu.SemaphoreType.DMA,
        ],
        compiler_params=params(),
        cost_estimate=cost(10**9 if n == NF else 10**8, 10 * 10**6),
    )(r, p, w, jac, weights, *faces)


def to_coarse(r, faces, restrict, jac, weights, diag, layers):
    e_total = r.shape[0]
    span = e_total // layers
    small = weights.shape[0] // 2
    n = NC
    group = 4

    def body(r_in, h1, h2, g1, g2, rest_ref, jac_ref, w_mat, diag_ref, rc_ref, u_ref, w_ref, c1, c2, z1, z2, r_fine, count_ref):
        count_ref[...] = half_faces(n, small)
        add_halo(NF, e_total, span, lambda e: r_in[e], r_fine, h1, h2, g1, g2)

        def some(i, carry):
            first = i * group
            wide = jnp.concatenate([r_fine[first + j] for j in range(group)], axis=1)
            product = times(rest_ref[...], wide)
            for j in range(group):
                rc_ref[first + j] = product[:, j * LANES : (j + 1) * LANES]
            return carry

        lax.fori_loop(0, e_total // group, some, 0, unroll=2)

        def u_of(e, r_here):
            w_here = DAMPING / (jac_ref[pl.ds(e, 1), :] * diag_ref[...] + count_ref[...])
            w_ref[e] = w_here
            return r_here * w_here

        correct(n, e_total, span, rc_ref, u_ref, u_of, c1, c2, z1, z2)
        subtract_operator(n, e_total, span, rc_ref, u_ref, w_mat, jac_ref, count_ref)

    field = jax.ShapeDtypeStruct((e_total, small, LANES), F32)
    return pl.pallas_call(
        body,
        out_shape=[field, field, field] + face_shapes(n, layers),
        scratch_shapes=[pltpu.VMEM(r.shape, F32), pltpu.VMEM((small, LANES), F32)],
        compiler_params=params(),
        cost_estimate=cost(5 * 10**8, 5 * 10**6),
        name="to_coarse",
    )(r, *faces, restrict, jac, weights, diag)


def to_coarsest(r, faces, restrict, layers):
    e_total = r.shape[0]
    span = e_total // layers
    group = 4

    def body(r_in, h1, h2, g1, g2, rest_ref, out_ref, r_done, kept, sem):
        add_halo(NC, e_total, span, lambda e: r_in[e], r_done, h1, h2, g1, g2)

        def some(i, carry):
            first = i * group
            wide = jnp.concatenate([r_done[first + j] for j in range(group)], axis=1)
            product = times(rest_ref[...], wide)
            for j in range(group):
                kept[first + j] = product[:LAST, j * LANES : (j + 1) * LANES]
            return carry

        lax.fori_loop(0, e_total // group, some, 0, unroll=8)
        stores = []
        for e in range(e_total):
            c = pltpu.make_async_copy(kept.at[e], out_ref.at[:, e, :], sem)
            c.start()
            stores.append(c)
        for c in stores:
            c.wait()

    whole = pl.BlockSpec()
    return pl.pallas_call(
        body,
        out_shape=jax.ShapeDtypeStruct((LAST, e_total, LANES), F32),
        in_specs=[whole] * 6,
        out_specs=any_spec(),
        scratch_shapes=[
            pltpu.VMEM(r.shape, F32),
            pltpu.VMEM((e_total, LAST, LANES), F32),
            pltpu.SemaphoreType.DMA,
        ],
        compiler_params=params(),
        cost_estimate=cost(5 * 10**7, 10**6),
        name="to_coarsest",
    )(r, *faces, restrict)


def move(x, axis, by):
    count = lax.axis_size(axis)
    return lax.ppermute(x, axis, [(i, (i + by) % count) for i in range(count)])


def swap(x, axis, odd_first):
    count = lax.axis_size(axis)
    pairs = []
    for i in range(count):
        ahead = (i % 2 == 0) != odd_first
        pairs.append((i, (i + 1) % count if ahead else (i - 1) % count))
    return lax.ppermute(x, axis, pairs)


def swap_inner(x, axis, other):
    count, beside = lax.axis_size(axis), lax.axis_size(other)
    pairs = []
    for j in range(beside):
        for i in range(count):
            to = i + 1 if i % 2 else i - 1
            target = (j, to) if 0 <= to < count else (j ^ 1, i)
            pairs.append((j * count + i, target[0] * count + target[1]))
    return lax.ppermute(x, (other, axis), pairs)


def exchange(faces):
    c1, c2, z1, z2 = faces
    c2 = swap(c2, "sector", True)
    z2 = swap_inner(z2, "block", "sector")
    z1 = swap(z1, "block", False)
    c1 = swap(c1, "sector", False)
    return c1, c2, z1, z2


def windows(pair, offsets, own):
    span = pair.shape[0] // 2
    buckets = span // STEP
    _, steps = turn_plan(offsets[0], span)

    def branch(number):
        by, bucket = number // buckets, number % buckets
        many, few = span - STEP * bucket, STEP * (bucket + 1)

        def run(pair, offsets, own):
            far, near, near_back, far_back = cut(pair, many, few)
            near = move(near, "sector", by)
            far = move(far, "sector", by + 1)
            near_back = move(near_back, "sector", -by)
            far_back = move(far_back, "sector", -by - 1)
            kept, w = own_part(offsets, pair, *own)
            return kept, w, join(far, near, near_back, far_back)

        return run

    branches = [branch(i) for i in range(lax.axis_size("sector") // 2 * buckets)]
    return lax.switch(lax.div(steps, STEP), branches, pair, offsets, own)


def per_device(
    source, jacobian, stiff_fine, stiff_coarse, restrict_fine, restrict_coarse, mortar_proj, rotor_trace,
    stator_trace, offsets,
):
    layers, span, axial = jacobian.shape
    e_total = layers * span
    source_rows = source.reshape(source.shape[0], e_total, axial)
    jac = jacobian.reshape(e_total, axial)
    rotor_rows = rotor_trace.reshape(-1, span, axial)
    stator_rows = stator_trace.reshape(-1, span, axial)
    pair, near1, near2, proj, back, wf, wc, rfs, rcs, df, dc = prepare(
        offsets, rotor_rows, stator_rows, mortar_proj.transpose(1, 0, 2),
        stiff_fine, stiff_coarse, restrict_fine, restrict_coarse,
    )
    near2 = swap(near2, "sector", True)
    near1 = swap(near1, "sector", False)
    kept, w, wins = windows(pair, offsets, (proj, jac, df))
    sflux, rflux, r, p, *faces = first_sweep(
        offsets, wins, pair, kept, near1, near2, proj, back, source_rows, w, jac, wf, layers
    )
    p, r, *faces = sweep(NF, r, p, w, jac, wf, exchange(faces), layers, False)
    fine, r, *faces = sweep(NF, r, p, w, jac, wf, exchange(faces), layers, True)
    r, p, w, *faces = to_coarse(r, exchange(faces), rfs, jac, wc, dc, layers)
    p, r, *faces = sweep(NC, r, p, w, jac, wc, exchange(faces), layers, False)
    coarse, r, *faces = sweep(NC, r, p, w, jac, wc, exchange(faces), layers, True)
    coarsest = to_coarsest(r, exchange(faces), rcs, layers)
    shape = (layers, span, axial)
    return (
        sflux.reshape(stator_trace.shape),
        rflux.reshape(rotor_trace.shape),
        fine.reshape((-1,) + shape),
        coarse.reshape((-1,) + shape),
        coarsest.reshape((-1,) + shape),
    )


def solution(mesh):
    cell = P(None, None, "sector", "block")

    return jax.shard_map(
        per_device,
        mesh=mesh,
        in_specs=(cell, P(None, "sector", "block"), P(), P(), P(), P(), P(), cell, cell, P("block")),
        out_specs=(cell,) * 5,
        check_vma=False,
    )
```

profile of v0, /device:TPU:0, one launch (start us, length us, event | category | flops | bytes accessed | tf_op | source)
XLA Modules:
  0.0 106.8 jit_solution(5249045201491440959)
XLA Ops:
  1.3 3.5 %prepare.1 = (f32[32,104,128]{2,1,0:T(8,128)}, f32[1,104,128]{2,1,0:T(8,128)S(1)}, f32[1,104,128]{2,1,0:T(8,128)S(1)}, bf16[416,224]{1,0:T(8,128)(2,1)S(1)}, bf1...) custom-call(s32[1]{0:T(128)} %copy.111.offset_ref, ...), custom_call_target="tpu_custom_call" | custom-call | tf_op jit(solution)/shard_map/prepare/pallas_call | solution.py:283
  4.8 0.6 collective-permute-start.128
  5.3 15.0 %conditional.1 = (f32[17,104,128]{2,1,0:T(8,128)}, f32[32,128,128]{2,1,0:T(8,128)S(1)}, f32[36,104,128]{2,1,0:T(8,128)S(1)}) conditional(s32[]{:T(128)} %clamp.3, (s32[1]{0:T(128)}, f32[32,104,128]{2,1,0:T(8,128)}, bf16[416,224]{1,0:T(8,128)(2,1)S(1)}, f32[32,128]{1,0:T(8,128)}, f32[128,128]{1,0:T(8,128)S(1)}) %tuple.188, ...), branch_computations={%region_0.1_spmd, %region_1.2_spmd, %region_2.3_spmd, %region_3.4_... | conditional | flops 2000000000 | bytes 17667896 | solution.py:699
  5.3 1.7 %cut.35 = (f32[8,104,128]{2,1,0:T(8,128)S(1)}, f32[10,104,128]{2,1,0:T(8,128)S(1)}, f32[10,104,128]{2,1,0:T(8,128)S(1)}, f32[8,104,128]{2,1,0:T(8,128)S(1)}) custom-call(f32[32,104,128]{2,1,0:T(8,128)} %get-tuple-element.354.pair_ref), custom_call_target="tpu_custom_call" | custom-call | tf_op jit(solution)/shard_map/cond/branch_3_fun/cut/pallas_call | solution.py:388
  7.0 0.0 collective-permute-start.13
  7.1 0.1 collective-permute-start.12
  7.2 3.5 %collective-permute-start.15 = (f32[8,104,128]{2,1,0:T(8,128)S(1)}, f32[8,104,128]{2,1,0:T(8,128)S(1)}, u32[]{:S(2)}, u32[]{:S(2)}) collective-permute-start(f32[8,104,128]{2,1,0:T(8,128)S(1)} %get-tuple-element.363), channel_id=1, source_target_pairs={{0,28},{4,0},{8,4},{12,8},{16,12},{20,16},{24,20},{28,24},{1,29},{... | collective-permute-start | bytes 1277960 | tf_op jit(solution)/shard_map/cond/branch_3_fun/ppermute | solution.py:646
  10.7 4.9 %own_part.35 = (f32[17,104,128]{2,1,0:T(8,128)}, f32[32,128,128]{2,1,0:T(8,128)S(1)}) custom-call(s32[1]{0:T(128)} %get-tuple-element.353.offset_ref, f32[32,104,128]{2,1,0:T(8,128)} %get-tuple-element.354.pair_ref, bf16[416,224]{1,0:T(8,128)(2,1)S(1)} %get-tuple-element.355.proj_ref, f32[32,128]{1,0:T(8,128)} %get-tuple-element.356.jac_ref, ...), custom_call_target="tpu_custom_call" | custom-call | flops 2000000000 | bytes 10000000 | tf_op jit(solution)/shard_map/cond/branch_3_fun/own_part/pallas_call | solution.py:356
  15.7 3.4 %collective-permute-done.12.far_ref = f32[8,104,128]{2,1,0:T(8,128)S(1)} collective-permute-done((f32[8,104,128]{2,1,0:T(8,128)S(1)}, f32[8,104,128]{2,1,0:T(8,128)S(1)}, u32[]{:S(2)}, u32[]{:S(2)}) %collective-permute-start.12) | collective-permute-done | bytes 426016 | tf_op jit(solution)/shard_map/cond/branch_3_fun/ppermute | solution.py:646
  19.0 0.3 collective-permute-done.15.far_back_ref
  19.3 0.6 join.35
  20.3 2.9 %collective-permute-start.129 = (f32[1,104,128]{2,1,0:T(8,128)S(1)}, f32[1,104,128]{2,1,0:T(8,128)S(1)}, u32[]{:S(2)}, u32[]{:S(2)}) collective-permute-start(f32[1,104,128]{2,1,0:T(8,128)S(1)} %get-tuple-element.736), channel_id=1, source_target_pairs={{0,28},{4,8},{8,4},{12,16},{16,12},{20,24},{24,20},{28,0},{1,29},{... | collective-permute-start | bytes 159752 | tf_op jit(solution)/shard_map/ppermute | solution.py:655
  23.2 1.8 %collective-permute-done.129.near2_ref = f32[1,104,128]{2,1,0:T(8,128)S(1)} collective-permute-done((f32[1,104,128]{2,1,0:T(8,128)S(1)}, f32[1,104,128]{2,1,0:T(8,128)S(1)}, u32[]{:S(2)}, u32[]{:S(2)}) %collective-permute-start.129) | collective-permute-done | bytes 53280 | tf_op jit(solution)/shard_map/ppermute | solution.py:655
  25.0 7.6 %first_sweep.1 = (f32[100,16,128]{2,1,0:T(8,128)}, f32[100,16,128]{2,1,0:T(8,128)}, f32[32,128,128]{2,1,0:T(8,128)S(1)}, f32[32,128,128]{2,1,0:T(8,128)S(1)}, f3...) custom-call(s32[1]{0:T(128)} %copy.111.offset_ref, ...), custom_call_target="tpu_custom_call" | custom-call | flops 2000000000 | bytes 20000000 | tf_op jit(solution)/shard_map/first_sweep/pallas_call | solution.py:497
  32.6 1.2 %collective-permute-start.130 = (f32[2,25,128]{2,1,0:T(8,128)S(1)}, f32[2,25,128]{2,1,0:T(8,128)S(1)}, u32[]{:S(2)}, u32[]{:S(2)}) collective-permute-start(f32[2,25,128]{2,1,0:T(8,128)S(1)} %get-tuple-element.744), channel_id=1, source_target_pairs={{0,4},{4,0},{8,12},{12,8},{16,20},{20,16},{24,28},{28,24},{1,5},{5... | collective-permute-start | bytes 76808 | tf_op jit(solution)/shard_map/ppermute | solution.py:655
  33.9 1.5 %collective-permute-start.131 = (f32[2,25,128]{2,1,0:T(8,128)S(1)}, f32[2,25,128]{2,1,0:T(8,128)S(1)}, u32[]{:S(2)}, u32[]{:S(2)}) collective-permute-start(f32[2,25,128]{2,1,0:T(8,128)S(1)} %get-tuple-element.745), channel_id=1, source_target_pairs={{0,28},{4,8},{8,4},{12,16},{16,12},{20,24},{24,20},{28,0},{1,29},{... | collective-permute-start | bytes 76808 | tf_op jit(solution)/shard_map/ppermute | solution.py:655
  35.4 31.1 %collective-permute-start.132 = (f32[5,8,128]{2,1,0:T(8,128)S(1)}, f32[5,8,128]{2,1,0:T(8,128)S(1)}, u32[]{:S(2)}, u32[]{:S(2)}) collective-permute-start(f32[5,8,128]{2,1,0:T(8,128)S(1)} %get-tuple-element.746), channel_id=1, source_target_pairs={{0,1},{1,0},{2,3},{3,2},{4,5},{5,4},{6,7},{7,6},{8,9},{9,8},{10,11... | collective-permute-start | bytes 61448 | tf_op jit(solution)/shard_map/ppermute | solution.py:655
  66.5 1.8 %collective-permute-done.132.g1 = f32[5,8,128]{2,1,0:T(8,128)S(1)} collective-permute-done((f32[5,8,128]{2,1,0:T(8,128)S(1)}, f32[5,8,128]{2,1,0:T(8,128)S(1)}, u32[]{:S(2)}, u32[]{:S(2)}) %collective-permute-start.132) | collective-permute-done | bytes 20512 | tf_op jit(solution)/shard_map/ppermute | solution.py:655
  68.2 2.3 %shard_map.137 = (f32[32,128,128]{2,1,0:T(8,128)S(1)}, f32[32,128,128]{2,1,0:T(8,128)S(1)}, f32[2,25,128]{2,1,0:T(8,128)S(1)}, f32[2,25,128]{2,1,0:T(8,128)S(1)}...) custom-call(f32[32,128,128]{2,1,0:T(8,128)S(1)} %get-tuple-element.742.r_in, ...), custom_call_target="tpu_custom_call" | custom-call | flops 1000000000 | bytes 10000000 | tf_op jit(solution)/shard_map/pallas_call | solution.py:547
  70.5 0.1 collective-permute-start.134
  70.6 0.7 collective-permute-start.135
  71.3 2.1 %collective-permute-start.136 = (f32[5,8,128]{2,1,0:T(8,128)S(1)}, f32[5,8,128]{2,1,0:T(8,128)S(1)}, u32[]{:S(2)}, u32[]{:S(2)}) collective-permute-start(f32[5,8,128]{2,1,0:T(8,128)S(1)} %get-tuple-element.752), channel_id=1, source_target_pairs={{0,1},{1,0},{2,3},{3,2},{4,5},{5,4},{6,7},{7,6},{8,9},{9,8},{10,11... | collective-permute-start | bytes 61448 | tf_op jit(solution)/shard_map/ppermute | solution.py:655
  73.4 1.8 %collective-permute-done.136.g1 = f32[5,8,128]{2,1,0:T(8,128)S(1)} collective-permute-done((f32[5,8,128]{2,1,0:T(8,128)S(1)}, f32[5,8,128]{2,1,0:T(8,128)S(1)}, u32[]{:S(2)}, u32[]{:S(2)}) %collective-permute-start.136) | collective-permute-done | bytes 20512 | tf_op jit(solution)/shard_map/ppermute | solution.py:655
  75.2 2.4 %shard_map.138 = (f32[125,32,128]{2,1,0:T(8,128)}, f32[32,128,128]{2,1,0:T(8,128)S(1)}, f32[2,25,128]{2,1,0:T(8,128)S(1)}, f32[2,25,128]{2,1,0:T(8,128)S(1)}, f3...) custom-call(f32[32,128,128]{2,1,0:T(8,128)S(1)} %get-tuple-element.748.r_in, ...), custom_call_target="tpu_custom_call" | custom-call | flops 1000000000 | bytes 10000000 | tf_op jit(solution)/shard_map/pallas_call | solution.py:547
  77.6 0.1 collective-permute-start.138
  77.7 1.8 %collective-permute-start.139 = (f32[2,25,128]{2,1,0:T(8,128)S(1)}, f32[2,25,128]{2,1,0:T(8,128)S(1)}, u32[]{:S(2)}, u32[]{:S(2)}) collective-permute-start(f32[2,25,128]{2,1,0:T(8,128)S(1)} %get-tuple-element.757), channel_id=1, source_target_pairs={{0,28},{4,8},{8,4},{12,16},{16,12},{20,24},{24,20},{28,0},{1,29},{... | collective-permute-start | bytes 76808 | tf_op jit(solution)/shard_map/ppermute | solution.py:655
  79.5 1.9 %collective-permute-start.140 = (f32[5,8,128]{2,1,0:T(8,128)S(1)}, f32[5,8,128]{2,1,0:T(8,128)S(1)}, u32[]{:S(2)}, u32[]{:S(2)}) collective-permute-start(f32[5,8,128]{2,1,0:T(8,128)S(1)} %get-tuple-element.758), channel_id=1, source_target_pairs={{0,1},{1,0},{2,3},{3,2},{4,5},{5,4},{6,7},{7,6},{8,9},{9,8},{10,11... | collective-permute-start | bytes 61448 | tf_op jit(solution)/shard_map/ppermute | solution.py:655
  81.4 1.9 %collective-permute-done.140.g1 = f32[5,8,128]{2,1,0:T(8,128)S(1)} collective-permute-done((f32[5,8,128]{2,1,0:T(8,128)S(1)}, f32[5,8,128]{2,1,0:T(8,128)S(1)}, u32[]{:S(2)}, u32[]{:S(2)}) %collective-permute-start.140) | collective-permute-done | bytes 20512 | tf_op jit(solution)/shard_map/ppermute | solution.py:655
  83.3 2.2 %to_coarse.1 = (f32[32,32,128]{2,1,0:T(8,128)S(1)}, f32[32,32,128]{2,1,0:T(8,128)S(1)}, f32[32,32,128]{2,1,0:T(8,128)S(1)}, f32[2,9,128]{2,1,0:T(8,128)S(1)}, f3...) custom-call(f32[32,128,128]{2,1,0:T(8,128)S(1)} %get-tuple-element.755.r_in, ...), custom_call_target="tpu_custom_call" | custom-call | flops 500000000 | bytes 5000000 | tf_op jit(solution)/shard_map/to_coarse/pallas_call | solution.py:592
  85.5 2.1 %collective-permute-start.144 = (f32[3,8,128]{2,1,0:T(8,128)S(1)}, f32[3,8,128]{2,1,0:T(8,128)S(1)}, u32[]{:S(2)}, u32[]{:S(2)}) collective-permute-start(f32[3,8,128]{2,1,0:T(8,128)S(1)} %get-tuple-element.768), channel_id=1, source_target_pairs={{0,1},{1,0},{2,3},{3,2},{4,5},{5,4},{6,7},{7,6},{8,9},{9,8},{10,11... | collective-permute-start | bytes 36872 | tf_op jit(solution)/shard_map/ppermute | solution.py:655
  87.6 0.5 collective-permute-start.142
  88.1 0.6 collective-permute-start.143
  88.8 0.2 collective-permute-done.142.h1
  89.0 3.2 %collective-permute-done.143.h2 = f32[2,9,128]{2,1,0:T(8,128)S(1)} collective-permute-done((f32[2,9,128]{2,1,0:T(8,128)S(1)}, f32[2,9,128]{2,1,0:T(8,128)S(1)}, u32[]{:S(2)}, u32[]{:S(2)}) %collective-permute-start.143) | collective-permute-done | bytes 9248 | tf_op jit(solution)/shard_map/ppermute | solution.py:655
  92.2 1.2 %shard_map.139 = (f32[32,32,128]{2,1,0:T(8,128)S(1)}, f32[32,32,128]{2,1,0:T(8,128)S(1)}, f32[2,9,128]{2,1,0:T(8,128)S(1)}, f32[2,9,128]{2,1,0:T(8,128)S(1)}, f3...) custom-call(f32[32,32,128]{2,1,0:T(8,128)S(1)} %get-tuple-element.763.r_in, f32[32,32,128]{2,1,0:T(8,128)S(1)} %get-tuple-element.764.p_in, ...), custom_call_target="tpu_custom_call" | custom-call | flops 100000000 | bytes 10000000 | tf_op jit(solution)/shard_map/pallas_call | solution.py:547
  93.4 0.1 collective-permute-start.148
  93.4 0.1 collective-permute-start.149
  93.5 0.5 collective-permute-start.146
  94.0 0.6 collective-permute-start.147
  94.7 0.2 collective-permute-done.146.h1
  94.8 3.3 %collective-permute-done.147.h2 = f32[2,9,128]{2,1,0:T(8,128)S(1)} collective-permute-done((f32[2,9,128]{2,1,0:T(8,128)S(1)}, f32[2,9,128]{2,1,0:T(8,128)S(1)}, u32[]{:S(2)}, u32[]{:S(2)}) %collective-permute-start.147) | collective-permute-done | bytes 9248 | tf_op jit(solution)/shard_map/ppermute | solution.py:655
  98.1 1.2 %shard_map.140 = (f32[27,32,128]{2,1,0:T(8,128)}, f32[32,32,128]{2,1,0:T(8,128)S(1)}, f32[2,9,128]{2,1,0:T(8,128)S(1)}, f32[2,9,128]{2,1,0:T(8,128)S(1)}, f32[3,...) custom-call(f32[32,32,128]{2,1,0:T(8,128)S(1)} %get-tuple-element.770.r_in, f32[32,32,128]{2,1,0:T(8,128)S(1)} %get-tuple-element.771.p_in, ...), custom_call_target="tpu_custom_call" | custom-call | flops 100000000 | bytes 10000000 | tf_op jit(solution)/shard_map/pallas_call | solution.py:547
  99.3 1.5 %collective-permute-start.152 = (f32[3,8,128]{2,1,0:T(8,128)S(1)}, f32[3,8,128]{2,1,0:T(8,128)S(1)}, u32[]{:S(2)}, u32[]{:S(2)}) collective-permute-start(f32[3,8,128]{2,1,0:T(8,128)S(1)} %get-tuple-element.780), channel_id=1, source_target_pairs={{0,1},{1,0},{2,3},{3,2},{4,5},{5,4},{6,7},{7,6},{8,9},{9,8},{10,11... | collective-permute-start | bytes 36872 | tf_op jit(solution)/shard_map/ppermute | solution.py:655
  100.8 0.5 collective-permute-start.150
  101.3 0.2 collective-permute-start.151
  101.6 0.6 collective-permute-done.150.h1
  102.2 3.2 %collective-permute-done.151.h2 = f32[2,9,128]{2,1,0:T(8,128)S(1)} collective-permute-done((f32[2,9,128]{2,1,0:T(8,128)S(1)}, f32[2,9,128]{2,1,0:T(8,128)S(1)}, u32[]{:S(2)}, u32[]{:S(2)}) %collective-permute-start.151) | collective-permute-done | bytes 9248 | tf_op jit(solution)/shard_map/ppermute | solution.py:655
  105.4 1.2 %to_coarsest.1 = f32[8,32,128]{2,1,0:T(8,128)} custom-call(f32[32,32,128]{2,1,0:T(8,128)S(1)} %get-tuple-element.777.r_in, f32[2,9,128]{2,1,0:T(8,128)S(1)} %collective-permute-done.150.h1, f32[2,9,128]{2,1,0:T(8,128)S(1)} %collective-permute-done.151.h2, f32[3,8,128]{2,1,0:T(8,128)S(1)} %collective-permute-done.152.g1, ...), custom_call_target="tpu_custom_call" | custom-call | flops 50000000 | bytes 1000000 | tf_op jit(solution)/shard_map/to_coarsest/pallas_call | solution.py:628
  (28 shorter events, 0.1 us)
Async XLA Ops:
  4.8 18.4 %collective-permute-start.128 = (f32[1,104,128]{2,1,0:T(8,128)S(1)}, f32[1,104,128]{2,1,0:T(8,128)S(1)}, u32[]{:S(2)}, u32[]{:S(2)}) collective-permute-start(f32[1,104,128]{2,1,0:T(8,128)S(1)} %get-tuple-element.735), channel_id=1, source_target_pairs={{0,4},{4,0},{8,12},{12,8},{16,20},{20,16},{24,28},{28,24},{1,5},{5... | collective-permute-start | bytes 159752 | tf_op jit(solution)/shard_map/ppermute | solution.py:655
  7.0 12.3 %collective-permute-start.13 = (f32[10,104,128]{2,1,0:T(8,128)S(1)}, f32[10,104,128]{2,1,0:T(8,128)S(1)}, u32[]{:S(2)}, u32[]{:S(2)}) collective-permute-start(f32[10,104,128]{2,1,0:T(8,128)S(1)} %get-tuple-element.361), channel_id=1, source_target_pairs={{0,0},{4,4},{8,8},{12,12},{16,16},{20,20},{24,24},{28,28},{1,1},{5... | collective-permute-start | bytes 1597448 | tf_op jit(solution)/shard_map/cond/branch_3_fun/ppermute | solution.py:646
  7.0 12.3 %collective-permute-start.14 = (f32[10,104,128]{2,1,0:T(8,128)S(1)}, f32[10,104,128]{2,1,0:T(8,128)S(1)}, u32[]{:S(2)}, u32[]{:S(2)}) collective-permute-start(f32[10,104,128]{2,1,0:T(8,128)S(1)} %get-tuple-element.362), channel_id=1, source_target_pairs={{0,0},{4,4},{8,8},{12,12},{16,16},{20,20},{24,24},{28,28},{1,1},{5... | collective-permute-start | bytes 1597448 | tf_op jit(solution)/shard_map/cond/branch_3_fun/ppermute | solution.py:646
  7.1 12.0 %collective-permute-start.12 = (f32[8,104,128]{2,1,0:T(8,128)S(1)}, f32[8,104,128]{2,1,0:T(8,128)S(1)}, u32[]{:S(2)}, u32[]{:S(2)}) collective-permute-start(f32[8,104,128]{2,1,0:T(8,128)S(1)} %get-tuple-element.360), channel_id=1, source_target_pairs={{0,4},{4,8},{8,12},{12,16},{16,20},{20,24},{24,28},{28,0},{1,5},{5... | collective-permute-start | bytes 1277960 | tf_op jit(solution)/shard_map/cond/branch_3_fun/ppermute | solution.py:646
  7.2 12.1 %collective-permute-start.15 = (f32[8,104,128]{2,1,0:T(8,128)S(1)}, f32[8,104,128]{2,1,0:T(8,128)S(1)}, u32[]{:S(2)}, u32[]{:S(2)}) collective-permute-start(f32[8,104,128]{2,1,0:T(8,128)S(1)} %get-tuple-element.363), channel_id=1, source_target_pairs={{0,28},{4,0},{8,4},{12,8},{16,12},{20,16},{24,20},{28,24},{1,29},{... | collective-permute-start | bytes 1277960 | tf_op jit(solution)/shard_map/cond/branch_3_fun/ppermute | solution.py:646
  20.3 4.7 %copy-start = (f32[36,104,128]{2,1,0:T(8,128)}, f32[36,104,128]{2,1,0:T(8,128)S(1)}, u32[]{:S(2)}) copy-start(f32[36,104,128]{2,1,0:T(8,128)S(1)} %get-tuple-element.733.wins_in) | copy-start | bytes 5750788
  20.3 4.7 %collective-permute-start.129 = (f32[1,104,128]{2,1,0:T(8,128)S(1)}, f32[1,104,128]{2,1,0:T(8,128)S(1)}, u32[]{:S(2)}, u32[]{:S(2)}) collective-permute-start(f32[1,104,128]{2,1,0:T(8,128)S(1)} %get-tuple-element.736), channel_id=1, source_target_pairs={{0,28},{4,8},{8,4},{12,16},{16,12},{20,24},{24,20},{28,0},{1,29},{... | collective-permute-start | bytes 159752 | tf_op jit(solution)/shard_map/ppermute | solution.py:655
  25.0 43.2 %copy-start.1 = (f32[2,16,128]{2,1,0:T(8,128)S(1)}, f32[2,16,128]{2,1,0:T(8,128)}, u32[]{:S(2)}) copy-start(f32[2,16,128]{2,1,0:T(8,128)} %param.43) | copy-start | bytes 49156
  32.6 35.6 %collective-permute-start.130 = (f32[2,25,128]{2,1,0:T(8,128)S(1)}, f32[2,25,128]{2,1,0:T(8,128)S(1)}, u32[]{:S(2)}, u32[]{:S(2)}) collective-permute-start(f32[2,25,128]{2,1,0:T(8,128)S(1)} %get-tuple-element.744), channel_id=1, source_target_pairs={{0,4},{4,0},{8,12},{12,8},{16,20},{20,16},{24,28},{28,24},{1,5},{5... | collective-permute-start | bytes 76808 | tf_op jit(solution)/shard_map/ppermute | solution.py:655
  33.9 34.4 %collective-permute-start.131 = (f32[2,25,128]{2,1,0:T(8,128)S(1)}, f32[2,25,128]{2,1,0:T(8,128)S(1)}, u32[]{:S(2)}, u32[]{:S(2)}) collective-permute-start(f32[2,25,128]{2,1,0:T(8,128)S(1)} %get-tuple-element.745), channel_id=1, source_target_pairs={{0,28},{4,8},{8,4},{12,16},{16,12},{20,24},{24,20},{28,0},{1,29},{... | collective-permute-start | bytes 76808 | tf_op jit(solution)/shard_map/ppermute | solution.py:655
  35.4 32.8 %collective-permute-start.132 = (f32[5,8,128]{2,1,0:T(8,128)S(1)}, f32[5,8,128]{2,1,0:T(8,128)S(1)}, u32[]{:S(2)}, u32[]{:S(2)}) collective-permute-start(f32[5,8,128]{2,1,0:T(8,128)S(1)} %get-tuple-element.746), channel_id=1, source_target_pairs={{0,1},{1,0},{2,3},{3,2},{4,5},{5,4},{6,7},{7,6},{8,9},{9,8},{10,11... | collective-permute-start | bytes 61448 | tf_op jit(solution)/shard_map/ppermute | solution.py:655
  66.5 1.8 %collective-permute-start.133 = (f32[5,8,128]{2,1,0:T(8,128)S(1)}, f32[5,8,128]{2,1,0:T(8,128)S(1)}, u32[]{:S(2)}, u32[]{:S(2)}) collective-permute-start(f32[5,8,128]{2,1,0:T(8,128)S(1)} %get-tuple-element.747), channel_id=1, source_target_pairs={{0,4},{1,2},{2,1},{3,7},{4,0},{5,6},{6,5},{7,3},{8,12},{9,10},{10,... | collective-permute-start | bytes 61448 | tf_op jit(solution)/shard_map/ppermute | solution.py:666
  70.5 4.7 %collective-permute-start.134 = (f32[2,25,128]{2,1,0:T(8,128)S(1)}, f32[2,25,128]{2,1,0:T(8,128)S(1)}, u32[]{:S(2)}, u32[]{:S(2)}) collective-permute-start(f32[2,25,128]{2,1,0:T(8,128)S(1)} %get-tuple-element.750), channel_id=1, source_target_pairs={{0,4},{4,0},{8,12},{12,8},{16,20},{20,16},{24,28},{28,24},{1,5},{5... | collective-permute-start | bytes 76808 | tf_op jit(solution)/shard_map/ppermute | solution.py:655
  70.6 4.6 %collective-permute-start.135 = (f32[2,25,128]{2,1,0:T(8,128)S(1)}, f32[2,25,128]{2,1,0:T(8,128)S(1)}, u32[]{:S(2)}, u32[]{:S(2)}) collective-permute-start(f32[2,25,128]{2,1,0:T(8,128)S(1)} %get-tuple-element.751), channel_id=1, source_target_pairs={{0,28},{4,8},{8,4},{12,16},{16,12},{20,24},{24,20},{28,0},{1,29},{... | collective-permute-start | bytes 76808 | tf_op jit(solution)/shard_map/ppermute | solution.py:655
  71.3 3.9 %collective-permute-start.136 = (f32[5,8,128]{2,1,0:T(8,128)S(1)}, f32[5,8,128]{2,1,0:T(8,128)S(1)}, u32[]{:S(2)}, u32[]{:S(2)}) collective-permute-start(f32[5,8,128]{2,1,0:T(8,128)S(1)} %get-tuple-element.752), channel_id=1, source_target_pairs={{0,1},{1,0},{2,3},{3,2},{4,5},{5,4},{6,7},{7,6},{8,9},{9,8},{10,11... | collective-permute-start | bytes 61448 | tf_op jit(solution)/shard_map/ppermute | solution.py:655
  73.4 1.8 %collective-permute-start.137 = (f32[5,8,128]{2,1,0:T(8,128)S(1)}, f32[5,8,128]{2,1,0:T(8,128)S(1)}, u32[]{:S(2)}, u32[]{:S(2)}) collective-permute-start(f32[5,8,128]{2,1,0:T(8,128)S(1)} %get-tuple-element.753), channel_id=1, source_target_pairs={{0,4},{1,2},{2,1},{3,7},{4,0},{5,6},{6,5},{7,3},{8,12},{9,10},{10,... | collective-permute-start | bytes 61448 | tf_op jit(solution)/shard_map/ppermute | solution.py:666
  77.6 5.7 %collective-permute-start.138 = (f32[2,25,128]{2,1,0:T(8,128)S(1)}, f32[2,25,128]{2,1,0:T(8,128)S(1)}, u32[]{:S(2)}, u32[]{:S(2)}) collective-permute-start(f32[2,25,128]{2,1,0:T(8,128)S(1)} %get-tuple-element.756), channel_id=1, source_target_pairs={{0,4},{4,0},{8,12},{12,8},{16,20},{20,16},{24,28},{28,24},{1,5},{5... | collective-permute-start | bytes 76808 | tf_op jit(solution)/shard_map/ppermute | solution.py:655
  77.7 5.6 %collective-permute-start.139 = (f32[2,25,128]{2,1,0:T(8,128)S(1)}, f32[2,25,128]{2,1,0:T(8,128)S(1)}, u32[]{:S(2)}, u32[]{:S(2)}) collective-permute-start(f32[2,25,128]{2,1,0:T(8,128)S(1)} %get-tuple-element.757), channel_id=1, source_target_pairs={{0,28},{4,8},{8,4},{12,16},{16,12},{20,24},{24,20},{28,0},{1,29},{... | collective-permute-start | bytes 76808 | tf_op jit(solution)/shard_map/ppermute | solution.py:655
  79.5 3.8 %collective-permute-start.140 = (f32[5,8,128]{2,1,0:T(8,128)S(1)}, f32[5,8,128]{2,1,0:T(8,128)S(1)}, u32[]{:S(2)}, u32[]{:S(2)}) collective-permute-start(f32[5,8,128]{2,1,0:T(8,128)S(1)} %get-tuple-element.758), channel_id=1, source_target_pairs={{0,1},{1,0},{2,3},{3,2},{4,5},{5,4},{6,7},{7,6},{8,9},{9,8},{10,11... | collective-permute-start | bytes 61448 | tf_op jit(solution)/shard_map/ppermute | solution.py:655
  81.4 1.9 %collective-permute-start.141 = (f32[5,8,128]{2,1,0:T(8,128)S(1)}, f32[5,8,128]{2,1,0:T(8,128)S(1)}, u32[]{:S(2)}, u32[]{:S(2)}) collective-permute-start(f32[5,8,128]{2,1,0:T(8,128)S(1)} %get-tuple-element.759), channel_id=1, source_target_pairs={{0,4},{1,2},{2,1},{3,7},{4,0},{5,6},{6,5},{7,3},{8,12},{9,10},{10,... | collective-permute-start | bytes 61448 | tf_op jit(solution)/shard_map/ppermute | solution.py:666
  85.5 6.7 %collective-permute-start.144 = (f32[3,8,128]{2,1,0:T(8,128)S(1)}, f32[3,8,128]{2,1,0:T(8,128)S(1)}, u32[]{:S(2)}, u32[]{:S(2)}) collective-permute-start(f32[3,8,128]{2,1,0:T(8,128)S(1)} %get-tuple-element.768), channel_id=1, source_target_pairs={{0,1},{1,0},{2,3},{3,2},{4,5},{5,4},{6,7},{7,6},{8,9},{9,8},{10,11... | collective-permute-start | bytes 36872 | tf_op jit(solution)/shard_map/ppermute | solution.py:655
  87.6 4.6 %collective-permute-start.145 = (f32[3,8,128]{2,1,0:T(8,128)S(1)}, f32[3,8,128]{2,1,0:T(8,128)S(1)}, u32[]{:S(2)}, u32[]{:S(2)}) collective-permute-start(f32[3,8,128]{2,1,0:T(8,128)S(1)} %get-tuple-element.769), channel_id=1, source_target_pairs={{0,4},{1,2},{2,1},{3,7},{4,0},{5,6},{6,5},{7,3},{8,12},{9,10},{10,... | collective-permute-start | bytes 36872 | tf_op jit(solution)/shard_map/ppermute | solution.py:666
  87.6 1.3 %collective-permute-start.142 = (f32[2,9,128]{2,1,0:T(8,128)S(1)}, f32[2,9,128]{2,1,0:T(8,128)S(1)}, u32[]{:S(2)}, u32[]{:S(2)}) collective-permute-start(f32[2,9,128]{2,1,0:T(8,128)S(1)} %get-tuple-element.766), channel_id=1, source_target_pairs={{0,4},{4,0},{8,12},{12,8},{16,20},{20,16},{24,28},{28,24},{1,5},{5... | collective-permute-start | bytes 27656 | tf_op jit(solution)/shard_map/ppermute | solution.py:655
  88.1 4.1 %collective-permute-start.143 = (f32[2,9,128]{2,1,0:T(8,128)S(1)}, f32[2,9,128]{2,1,0:T(8,128)S(1)}, u32[]{:S(2)}, u32[]{:S(2)}) collective-permute-start(f32[2,9,128]{2,1,0:T(8,128)S(1)} %get-tuple-element.767), channel_id=1, source_target_pairs={{0,28},{4,8},{8,4},{12,16},{16,12},{20,24},{24,20},{28,0},{1,29},{... | collective-permute-start | bytes 27656 | tf_op jit(solution)/shard_map/ppermute | solution.py:655
  93.4 4.8 %collective-permute-start.148 = (f32[3,8,128]{2,1,0:T(8,128)S(1)}, f32[3,8,128]{2,1,0:T(8,128)S(1)}, u32[]{:S(2)}, u32[]{:S(2)}) collective-permute-start(f32[3,8,128]{2,1,0:T(8,128)S(1)} %get-tuple-element.774), channel_id=1, source_target_pairs={{0,1},{1,0},{2,3},{3,2},{4,5},{5,4},{6,7},{7,6},{8,9},{9,8},{10,11... | collective-permute-start | bytes 36872 | tf_op jit(solution)/shard_map/ppermute | solution.py:655
  93.4 4.7 %collective-permute-start.149 = (f32[3,8,128]{2,1,0:T(8,128)S(1)}, f32[3,8,128]{2,1,0:T(8,128)S(1)}, u32[]{:S(2)}, u32[]{:S(2)}) collective-permute-start(f32[3,8,128]{2,1,0:T(8,128)S(1)} %get-tuple-element.775), channel_id=1, source_target_pairs={{0,4},{1,2},{2,1},{3,7},{4,0},{5,6},{6,5},{7,3},{8,12},{9,10},{10,... | collective-permute-start | bytes 36872 | tf_op jit(solution)/shard_map/ppermute | solution.py:666
  93.5 1.3 %collective-permute-start.146 = (f32[2,9,128]{2,1,0:T(8,128)S(1)}, f32[2,9,128]{2,1,0:T(8,128)S(1)}, u32[]{:S(2)}, u32[]{:S(2)}) collective-permute-start(f32[2,9,128]{2,1,0:T(8,128)S(1)} %get-tuple-element.772), channel_id=1, source_target_pairs={{0,4},{4,0},{8,12},{12,8},{16,20},{20,16},{24,28},{28,24},{1,5},{5... | collective-permute-start | bytes 27656 | tf_op jit(solution)/shard_map/ppermute | solution.py:655
  94.0 4.1 %collective-permute-start.147 = (f32[2,9,128]{2,1,0:T(8,128)S(1)}, f32[2,9,128]{2,1,0:T(8,128)S(1)}, u32[]{:S(2)}, u32[]{:S(2)}) collective-permute-start(f32[2,9,128]{2,1,0:T(8,128)S(1)} %get-tuple-element.773), channel_id=1, source_target_pairs={{0,28},{4,8},{8,4},{12,16},{16,12},{20,24},{24,20},{28,0},{1,29},{... | collective-permute-start | bytes 27656 | tf_op jit(solution)/shard_map/ppermute | solution.py:655
  99.3 6.1 %collective-permute-start.152 = (f32[3,8,128]{2,1,0:T(8,128)S(1)}, f32[3,8,128]{2,1,0:T(8,128)S(1)}, u32[]{:S(2)}, u32[]{:S(2)}) collective-permute-start(f32[3,8,128]{2,1,0:T(8,128)S(1)} %get-tuple-element.780), channel_id=1, source_target_pairs={{0,1},{1,0},{2,3},{3,2},{4,5},{5,4},{6,7},{7,6},{8,9},{9,8},{10,11... | collective-permute-start | bytes 36872 | tf_op jit(solution)/shard_map/ppermute | solution.py:655
  100.8 4.6 %collective-permute-start.153 = (f32[3,8,128]{2,1,0:T(8,128)S(1)}, f32[3,8,128]{2,1,0:T(8,128)S(1)}, u32[]{:S(2)}, u32[]{:S(2)}) collective-permute-start(f32[3,8,128]{2,1,0:T(8,128)S(1)} %get-tuple-element.781), channel_id=1, source_target_pairs={{0,4},{1,2},{2,1},{3,7},{4,0},{5,6},{6,5},{7,3},{8,12},{9,10},{10,... | collective-permute-start | bytes 36872 | tf_op jit(solution)/shard_map/ppermute | solution.py:666
  100.8 1.3 %collective-permute-start.150 = (f32[2,9,128]{2,1,0:T(8,128)S(1)}, f32[2,9,128]{2,1,0:T(8,128)S(1)}, u32[]{:S(2)}, u32[]{:S(2)}) collective-permute-start(f32[2,9,128]{2,1,0:T(8,128)S(1)} %get-tuple-element.778), channel_id=1, source_target_pairs={{0,4},{4,0},{8,12},{12,8},{16,20},{20,16},{24,28},{28,24},{1,5},{5... | collective-permute-start | bytes 27656 | tf_op jit(solution)/shard_map/ppermute | solution.py:655
  101.3 4.1 %collective-permute-start.151 = (f32[2,9,128]{2,1,0:T(8,128)S(1)}, f32[2,9,128]{2,1,0:T(8,128)S(1)}, u32[]{:S(2)}, u32[]{:S(2)}) collective-permute-start(f32[2,9,128]{2,1,0:T(8,128)S(1)} %get-tuple-element.779), channel_id=1, source_target_pairs={{0,28},{4,8},{8,4},{12,16},{16,12},{20,24},{24,20},{28,0},{1,29},{... | collective-permute-start | bytes 27656 | tf_op jit(solution)/shard_map/ppermute | solution.py:655
where the time goes:
time: 107 us
  starting transfers between devices  54.4 us (51%)
  Pallas kernels  28.7 us (27%)
  waiting for transfers between devices  21.7 us (20%)
  between operations  1.61 us (2%)
    ppermute x20, starting transfers between devices, swap(): return lax.ppermute(x, axis, pairs)  50.6 us
    ppermute x20, waiting for transfers between devices, swap(): return lax.ppermute(x, axis, pairs)  18 us
    pallas_call x1, Pallas kernels, first_sweep(): pl.pallas_call(body, out_shape=[trace, trace, field, field] + face_shapes...  7.58 us
    pallas_call x4, Pallas kernels, sweep(): pl.pallas_call(body, out_shape=[kept, field] + face_shapes(n, layers), ou...  7.05 us
    pallas_call x1, Pallas kernels, own_part(): pl.pallas_call(body, out_shape=[jax.ShapeDtypeStruct((span + 1, tall, LAN...  4.94 us
    ppermute x4, starting transfers between devices, move(): return lax.ppermute(x, axis, [(i, (i + by) % count) for i in range(count)])  3.73 us
    ppermute x4, waiting for transfers between devices, move(): return lax.ppermute(x, axis, [(i, (i + by) % count) for i in range(count)])  3.65 us
    pallas_call x1, Pallas kernels, prepare(): pl.pallas_call(body, out_shape=[jax.ShapeDtypeStruct((2 * span, tall, LAN...  3.48 us
  transfers between devices with their start and end apart: 30, of which 12 were waited for; matrix products, arithmetic and copies ran while one was open for 0% of the time, Pallas kernels for 7%

commit v1 on v0

--- a/solution.py
+++ b/solution.py
@@ -18,7 +18,7 @@
 HALO_UNROLL = 32
 GROUP = {NF: 4, NC: 16}
 GROUP_UNROLL = {NF: 4, NC: 1}
-VMEM_BYTES = 12 * 1024 * 1024
+VMEM_BYTES = 14 * 1024 * 1024
 
 
 def up(value, unit):
@@ -31,10 +31,6 @@
 
 def hbm_spec():
     return pl.BlockSpec(memory_space=pltpu.HBM)
-
-
-def in_vmem(array):
-    return pltpu.with_memory_space_constraint(array, pltpu.VMEM)
 
 
 def in_hbm(*arrays):
@@ -283,7 +279,7 @@
     return pl.pallas_call(
         body,
         out_shape=[
-            jax.ShapeDtypeStruct((2 * span, tall, LANES), F32),
+            pltpu.VMEM((2 * span, tall, LANES), F32),
             jax.ShapeDtypeStruct((1, tall, LANES), F32),
             jax.ShapeDtypeStruct((1, tall, LANES), F32),
             jax.ShapeDtypeStruct((4 * tall, 2 * wide), BF16),
@@ -372,7 +368,7 @@
         out[into + f] = source[first + f]
         return carry
 
-    lax.fori_loop(0, count, one, 0)
+    lax.fori_loop(0, count, one, 0, unroll=2)
 
 
 def cut(pair, many, few):
@@ -406,7 +402,7 @@
 
     return pl.pallas_call(
         body,
-        out_shape=jax.ShapeDtypeStruct((2 * reach,) + far.shape[1:], F32),
+        out_shape=pltpu.HBM((2 * reach,) + far.shape[1:], F32),
         out_specs=hbm_spec(),
         scratch_shapes=[pltpu.SemaphoreType.DMA],
         compiler_params=params(),
@@ -425,9 +421,9 @@
     height = weights.shape[0] // 2
 
     def body(
-        offset_ref, wins_in, pair_ref, kept_ref, near1_ref, near2_ref, proj_ref, back_ref, source_ref, w_ref,
+        offset_ref, wins_in, pair_ref, kept_ref, near1_ref, near2_ref, proj_ref, back_ref, source_ref, w_in,
         jac_ref, w_mat, sflux_out, rflux_out, r_ref, u_ref, c1, c2, z1, z2,
-        y0, y1, x0, x1, sflux, rflux, count_ref, wins_ref, in_sem, out_sem, win_sems,
+        y0, y1, x0, x1, sflux, rflux, count_ref, wins_ref, w_ref, in_sem, out_sem, win_sems,
     ):
         loads = [
             pltpu.make_async_copy(source_ref.at[:, e, :], r_ref.at[e, pl.ds(0, nodes), :], in_sem)
@@ -440,6 +436,7 @@
             pltpu.make_async_copy(wins_in.at[pl.ds(first, reach)], wins_ref.at[pl.ds(first, reach)], win_sems.at[k])
             for k, first in enumerate((rotor_half, reach - rotor_half))
         ]
+        loads.append(pltpu.make_async_copy(w_in, w_ref, win_sems.at[2]))
         for c in halves + loads:
             c.start()
         ahead, behind = STEP - 1 - inner, reach + inner
@@ -497,7 +494,7 @@
     return pl.pallas_call(
         body,
         out_shape=[trace, trace, field, field] + face_shapes(n, layers),
-        in_specs=[smem_spec(), hbm_spec()] + [whole] * 6 + [hbm_spec()] + [whole] * 3,
+        in_specs=[smem_spec(), hbm_spec()] + [whole] * 6 + [hbm_spec()] * 2 + [whole] * 2,
         out_specs=[hbm_spec()] * 2 + [whole] * 6,
         scratch_shapes=[slabs] * 4
         + [
@@ -505,14 +502,15 @@
             pltpu.VMEM((span, tall, LANES), F32),
             pltpu.VMEM((height, LANES), F32),
             pltpu.VMEM(wins.shape, F32),
+            pltpu.VMEM(w.shape, F32),
             pltpu.SemaphoreType.DMA,
             pltpu.SemaphoreType.DMA,
-            pltpu.SemaphoreType.DMA((2,)),
+            pltpu.SemaphoreType.DMA((3,)),
         ],
         compiler_params=params(),
         cost_estimate=cost(2 * 10**9, 20 * 10**6),
         name="first_sweep",
-    )(offsets, *in_hbm(wins), pair, kept, near1, near2, proj, back, *in_hbm(source), in_vmem(w), jac, weights)
+    )(offsets, *in_hbm(wins), pair, kept, near1, near2, proj, back, *in_hbm(source, w), jac, weights)
 
 
 def sweep(n, r, p, w, jac, weights, faces, layers, last):

time: 107 us -> 109 us (1.019)
  starting transfers between devices: 54.4 us -> 59.4 us
  Pallas kernels: 28.7 us -> 25.5 us
    ppermute x20, starting transfers between devices: 50.6 us -> 55.6 us  [swap(): return lax.ppermute(x, axis, pairs)]
    pallas_call x1, Pallas kernels: 1.65 us -> 0.16 us  [cut(): pl.pallas_call(body, out_shape=piece, compiler_params=params(), name='cut')]
  transfers between devices with their start and end apart: 30 -> 30, of which waited for: 12 -> 10; matrix products, arithmetic and copies ran while one was open for 0% -> 0% of each run, Pallas kernels for 7% -> 6%
where the time goes in v1:
time: 109 us; the launch traced here: 108 us
  starting transfers between devices  59.4 us (54%)
  Pallas kernels  25.5 us (23%)
  waiting for transfers between devices  21.6 us (20%)
  between operations  1.63 us (1%)
    ppermute x20, starting transfers between devices, swap(): return lax.ppermute(x, axis, pairs)  55.6 us
    ppermute x20, waiting for transfers between devices, swap(): return lax.ppermute(x, axis, pairs)  17.6 us
    pallas_call x4, Pallas kernels, sweep(): pl.pallas_call(body, out_shape=[kept, field] + face_shapes(n, layers), ou...  7.07 us
    pallas_call x1, Pallas kernels, first_sweep(): pl.pallas_call(body, out_shape=[trace, trace, field, field] + face_shapes...  6.69 us
    pallas_call x1, Pallas kernels, own_part(): pl.pallas_call(body, out_shape=[jax.ShapeDtypeStruct((span + 1, tall, LAN...  4.57 us
    ppermute x4, waiting for transfers between devices, move(): return lax.ppermute(x, axis, [(i, (i + by) % count) for i in range(count)])  4.01 us
    ppermute x4, starting transfers between devices, move(): return lax.ppermute(x, axis, [(i, (i + by) % count) for i in range(count)])  3.73 us
    pallas_call x1, Pallas kernels, prepare(): pl.pallas_call(body, out_shape=[pltpu.VMEM((2 * span, tall, LANES), F32),...  2.28 us
  transfers between devices with their start and end apart: 30, of which 10 were waited for; matrix products, arithmetic and copies ran while one was open for 0% of the time, Pallas kernels for 6%

profile of v1, /device:TPU:0, one launch (start us, length us, event | category | flops | bytes accessed | tf_op | source)
XLA Modules:
  0.0 108.4 jit_solution(13101161017761015913)
XLA Ops:
  1.3 2.3 %prepare.1 = (f32[32,104,128]{2,1,0:T(8,128)S(1)}, f32[1,104,128]{2,1,0:T(8,128)S(1)}, f32[1,104,128]{2,1,0:T(8,128)S(1)}, bf16[416,224]{1,0:T(8,128)(2,1)S(1)},...) custom-call(s32[1]{0:T(128)} %copy.111.offset_ref, ...), custom_call_target="tpu_custom_call" | custom-call | tf_op jit(solution)/shard_map/prepare/pallas_call | solution.py:279
  3.6 0.6 collective-permute-start.128
  4.1 14.0 %conditional.1 = (f32[17,104,128]{2,1,0:T(8,128)S(1)}, f32[32,128,128]{2,1,0:T(8,128)}, f32[36,104,128]{2,1,0:T(8,128)}) conditional(s32[]{:T(128)} %clamp.3, (s32[1]{0:T(128)}, f32[32,104,128]{2,1,0:T(8,128)S(1)}, bf16[416,224]{1,0:T(8,128)(2,1)S(1)}, f32[32,128]{1,0:T(8,128)}, f32[128,128]{1,0:T(8,128)S(1)}) %tuple.188, ...), branch_computations={%region_0.1_spmd, %region_1.2_spmd, %region_2.3_spmd, %region_3.4_... | conditional | flops 2000000000 | bytes 17667896 | solution.py:697
  4.1 0.2 cut.35
  4.3 0.0 collective-permute-start.13
  4.4 0.1 collective-permute-start.12
  4.5 3.5 %collective-permute-start.15 = (f32[8,104,128]{2,1,0:T(8,128)S(1)}, f32[8,104,128]{2,1,0:T(8,128)S(1)}, u32[]{:S(2)}, u32[]{:S(2)}) collective-permute-start(f32[8,104,128]{2,1,0:T(8,128)S(1)} %get-tuple-element.363), channel_id=1, source_target_pairs={{0,28},{4,0},{8,4},{12,8},{16,12},{20,16},{24,20},{28,24},{1,29},{... | collective-permute-start | bytes 1277960 | tf_op jit(solution)/shard_map/cond/branch_3_fun/ppermute | solution.py:644
  8.0 4.6 %own_part.35 = (f32[17,104,128]{2,1,0:T(8,128)S(1)}, f32[32,128,128]{2,1,0:T(8,128)}) custom-call(s32[1]{0:T(128)} %get-tuple-element.353.offset_ref, f32[32,104,128]{2,1,0:T(8,128)S(1)} %get-tuple-element.354.pair_ref, bf16[416,224]{1,0:T(8,128)(2,1)S(1)} %get-tuple-element.355.proj_ref, f32[32,128]{1,0:T(8,128)} %get-tuple-element.356.jac_ref, ...), custom_call_target="tpu_custom_call" | custom-call | flops 2000000000 | bytes 10000000 | tf_op jit(solution)/shard_map/cond/branch_3_fun/own_part/pallas_call | solution.py:352
  12.6 3.7 %collective-permute-done.12.far_ref = f32[8,104,128]{2,1,0:T(8,128)S(1)} collective-permute-done((f32[8,104,128]{2,1,0:T(8,128)S(1)}, f32[8,104,128]{2,1,0:T(8,128)S(1)}, u32[]{:S(2)}, u32[]{:S(2)}) %collective-permute-start.12) | collective-permute-done | bytes 426016 | tf_op jit(solution)/shard_map/cond/branch_3_fun/ppermute | solution.py:644
  16.3 0.3 collective-permute-done.15.far_back_ref
  16.6 1.3 %join.35 = f32[36,104,128]{2,1,0:T(8,128)} custom-call(f32[8,104,128]{2,1,0:T(8,128)S(1)} %collective-permute-done.12.far_ref, f32[10,104,128]{2,1,0:T(8,128)S(1)} %collective-permute-done.13.near_ref, f32[10,104,128]{2,1,0:T(8,128)S(1)} %collective-permute-done.14.near_back_ref, f32[8,104,128]{2,1,0:T(8,128)S(1)} %collective-permute-done.15.far_back_ref), custom_call_target="tpu_custom_call" | custom-call | tf_op jit(solution)/shard_map/cond/branch_3_fun/join/pallas_call | solution.py:403
  18.2 2.9 %collective-permute-start.129 = (f32[1,104,128]{2,1,0:T(8,128)S(1)}, f32[1,104,128]{2,1,0:T(8,128)S(1)}, u32[]{:S(2)}, u32[]{:S(2)}) collective-permute-start(f32[1,104,128]{2,1,0:T(8,128)S(1)} %get-tuple-element.736), channel_id=1, source_target_pairs={{0,28},{4,8},{8,4},{12,16},{16,12},{20,24},{24,20},{28,0},{1,29},{... | collective-permute-start | bytes 159752 | tf_op jit(solution)/shard_map/ppermute | solution.py:653
  21.1 1.8 %collective-permute-done.129.near2_ref = f32[1,104,128]{2,1,0:T(8,128)S(1)} collective-permute-done((f32[1,104,128]{2,1,0:T(8,128)S(1)}, f32[1,104,128]{2,1,0:T(8,128)S(1)}, u32[]{:S(2)}, u32[]{:S(2)}) %collective-permute-start.129) | collective-permute-done | bytes 53280 | tf_op jit(solution)/shard_map/ppermute | solution.py:653
  22.9 6.7 %first_sweep.1 = (f32[100,16,128]{2,1,0:T(8,128)}, f32[100,16,128]{2,1,0:T(8,128)}, f32[32,128,128]{2,1,0:T(8,128)S(1)}, f32[32,128,128]{2,1,0:T(8,128)S(1)}, f3...) custom-call(s32[1]{0:T(128)} %copy.111.offset_ref, ...), custom_call_target="tpu_custom_call" | custom-call | flops 2000000000 | bytes 20000000 | tf_op jit(solution)/shard_map/first_sweep/pallas_call | solution.py:494
  29.6 1.3 %collective-permute-start.130 = (f32[2,25,128]{2,1,0:T(8,128)S(1)}, f32[2,25,128]{2,1,0:T(8,128)S(1)}, u32[]{:S(2)}, u32[]{:S(2)}) collective-permute-start(f32[2,25,128]{2,1,0:T(8,128)S(1)} %get-tuple-element.744), channel_id=1, source_target_pairs={{0,4},{4,0},{8,12},{12,8},{16,20},{20,16},{24,28},{28,24},{1,5},{5... | collective-permute-start | bytes 76808 | tf_op jit(solution)/shard_map/ppermute | solution.py:653
  30.8 1.5 %collective-permute-start.131 = (f32[2,25,128]{2,1,0:T(8,128)S(1)}, f32[2,25,128]{2,1,0:T(8,128)S(1)}, u32[]{:S(2)}, u32[]{:S(2)}) collective-permute-start(f32[2,25,128]{2,1,0:T(8,128)S(1)} %get-tuple-element.745), channel_id=1, source_target_pairs={{0,28},{4,8},{8,4},{12,16},{16,12},{20,24},{24,20},{28,0},{1,29},{... | collective-permute-start | bytes 76808 | tf_op jit(solution)/shard_map/ppermute | solution.py:653
  32.3 35.7 %collective-permute-start.132 = (f32[5,8,128]{2,1,0:T(8,128)S(1)}, f32[5,8,128]{2,1,0:T(8,128)S(1)}, u32[]{:S(2)}, u32[]{:S(2)}) collective-permute-start(f32[5,8,128]{2,1,0:T(8,128)S(1)} %get-tuple-element.746), channel_id=1, source_target_pairs={{0,1},{1,0},{2,3},{3,2},{4,5},{5,4},{6,7},{7,6},{8,9},{9,8},{10,11... | collective-permute-start | bytes 61448 | tf_op jit(solution)/shard_map/ppermute | solution.py:653
  68.0 1.8 %collective-permute-done.132.g1 = f32[5,8,128]{2,1,0:T(8,128)S(1)} collective-permute-done((f32[5,8,128]{2,1,0:T(8,128)S(1)}, f32[5,8,128]{2,1,0:T(8,128)S(1)}, u32[]{:S(2)}, u32[]{:S(2)}) %collective-permute-start.132) | collective-permute-done | bytes 20512 | tf_op jit(solution)/shard_map/ppermute | solution.py:653
  69.8 2.3 %shard_map.137 = (f32[32,128,128]{2,1,0:T(8,128)S(1)}, f32[32,128,128]{2,1,0:T(8,128)S(1)}, f32[2,25,128]{2,1,0:T(8,128)S(1)}, f32[2,25,128]{2,1,0:T(8,128)S(1)}...) custom-call(f32[32,128,128]{2,1,0:T(8,128)S(1)} %get-tuple-element.742.r_in, ...), custom_call_target="tpu_custom_call" | custom-call | flops 1000000000 | bytes 10000000 | tf_op jit(solution)/shard_map/pallas_call | solution.py:545
  72.1 0.1 collective-permute-start.134
  72.2 0.7 collective-permute-start.135
  72.8 2.2 %collective-permute-start.136 = (f32[5,8,128]{2,1,0:T(8,128)S(1)}, f32[5,8,128]{2,1,0:T(8,128)S(1)}, u32[]{:S(2)}, u32[]{:S(2)}) collective-permute-start(f32[5,8,128]{2,1,0:T(8,128)S(1)} %get-tuple-element.752), channel_id=1, source_target_pairs={{0,1},{1,0},{2,3},{3,2},{4,5},{5,4},{6,7},{7,6},{8,9},{9,8},{10,11... | collective-permute-start | bytes 61448 | tf_op jit(solution)/shard_map/ppermute | solution.py:653
  75.0 1.8 %collective-permute-done.136.g1 = f32[5,8,128]{2,1,0:T(8,128)S(1)} collective-permute-done((f32[5,8,128]{2,1,0:T(8,128)S(1)}, f32[5,8,128]{2,1,0:T(8,128)S(1)}, u32[]{:S(2)}, u32[]{:S(2)}) %collective-permute-start.136) | collective-permute-done | bytes 20512 | tf_op jit(solution)/shard_map/ppermute | solution.py:653
  76.8 2.4 %shard_map.138 = (f32[125,32,128]{2,1,0:T(8,128)}, f32[32,128,128]{2,1,0:T(8,128)S(1)}, f32[2,25,128]{2,1,0:T(8,128)S(1)}, f32[2,25,128]{2,1,0:T(8,128)S(1)}, f3...) custom-call(f32[32,128,128]{2,1,0:T(8,128)S(1)} %get-tuple-element.748.r_in, ...), custom_call_target="tpu_custom_call" | custom-call | flops 1000000000 | bytes 10000000 | tf_op jit(solution)/shard_map/pallas_call | solution.py:545
  79.2 0.1 collective-permute-start.138
  79.3 1.8 %collective-permute-start.139 = (f32[2,25,128]{2,1,0:T(8,128)S(1)}, f32[2,25,128]{2,1,0:T(8,128)S(1)}, u32[]{:S(2)}, u32[]{:S(2)}) collective-permute-start(f32[2,25,128]{2,1,0:T(8,128)S(1)} %get-tuple-element.757), channel_id=1, source_target_pairs={{0,28},{4,8},{8,4},{12,16},{16,12},{20,24},{24,20},{28,0},{1,29},{... | collective-permute-start | bytes 76808 | tf_op jit(solution)/shard_map/ppermute | solution.py:653
  81.1 1.9 %collective-permute-start.140 = (f32[5,8,128]{2,1,0:T(8,128)S(1)}, f32[5,8,128]{2,1,0:T(8,128)S(1)}, u32[]{:S(2)}, u32[]{:S(2)}) collective-permute-start(f32[5,8,128]{2,1,0:T(8,128)S(1)} %get-tuple-element.758), channel_id=1, source_target_pairs={{0,1},{1,0},{2,3},{3,2},{4,5},{5,4},{6,7},{7,6},{8,9},{9,8},{10,11... | collective-permute-start | bytes 61448 | tf_op jit(solution)/shard_map/ppermute | solution.py:653
  83.0 1.9 %collective-permute-done.140.g1 = f32[5,8,128]{2,1,0:T(8,128)S(1)} collective-permute-done((f32[5,8,128]{2,1,0:T(8,128)S(1)}, f32[5,8,128]{2,1,0:T(8,128)S(1)}, u32[]{:S(2)}, u32[]{:S(2)}) %collective-permute-start.140) | collective-permute-done | bytes 20512 | tf_op jit(solution)/shard_map/ppermute | solution.py:653
  84.9 2.2 %to_coarse.1 = (f32[32,32,128]{2,1,0:T(8,128)S(1)}, f32[32,32,128]{2,1,0:T(8,128)S(1)}, f32[32,32,128]{2,1,0:T(8,128)S(1)}, f32[2,9,128]{2,1,0:T(8,128)S(1)}, f3...) custom-call(f32[32,128,128]{2,1,0:T(8,128)S(1)} %get-tuple-element.755.r_in, ...), custom_call_target="tpu_custom_call" | custom-call | flops 500000000 | bytes 5000000 | tf_op jit(solution)/shard_map/to_coarse/pallas_call | solution.py:590
  87.1 2.1 %collective-permute-start.144 = (f32[3,8,128]{2,1,0:T(8,128)S(1)}, f32[3,8,128]{2,1,0:T(8,128)S(1)}, u32[]{:S(2)}, u32[]{:S(2)}) collective-permute-start(f32[3,8,128]{2,1,0:T(8,128)S(1)} %get-tuple-element.768), channel_id=1, source_target_pairs={{0,1},{1,0},{2,3},{3,2},{4,5},{5,4},{6,7},{7,6},{8,9},{9,8},{10,11... | collective-permute-start | bytes 36872 | tf_op jit(solution)/shard_map/ppermute | solution.py:653
  89.1 0.5 collective-permute-start.142
  89.6 0.8 collective-permute-start.143
  90.4 0.0 collective-permute-done.142.h1
  90.5 3.2 %collective-permute-done.143.h2 = f32[2,9,128]{2,1,0:T(8,128)S(1)} collective-permute-done((f32[2,9,128]{2,1,0:T(8,128)S(1)}, f32[2,9,128]{2,1,0:T(8,128)S(1)}, u32[]{:S(2)}, u32[]{:S(2)}) %collective-permute-start.143) | collective-permute-done | bytes 9248 | tf_op jit(solution)/shard_map/ppermute | solution.py:653
  93.7 1.2 %shard_map.139 = (f32[32,32,128]{2,1,0:T(8,128)S(1)}, f32[32,32,128]{2,1,0:T(8,128)S(1)}, f32[2,9,128]{2,1,0:T(8,128)S(1)}, f32[2,9,128]{2,1,0:T(8,128)S(1)}, f3...) custom-call(f32[32,32,128]{2,1,0:T(8,128)S(1)} %get-tuple-element.763.r_in, f32[32,32,128]{2,1,0:T(8,128)S(1)} %get-tuple-element.764.p_in, ...), custom_call_target="tpu_custom_call" | custom-call | flops 100000000 | bytes 10000000 | tf_op jit(solution)/shard_map/pallas_call | solution.py:545
  94.9 0.1 collective-permute-start.148
  95.0 0.1 collective-permute-start.149
  95.0 0.5 collective-permute-start.146
  95.5 0.8 collective-permute-start.147
  96.3 0.1 collective-permute-done.146.h1
  96.4 3.3 %collective-permute-done.147.h2 = f32[2,9,128]{2,1,0:T(8,128)S(1)} collective-permute-done((f32[2,9,128]{2,1,0:T(8,128)S(1)}, f32[2,9,128]{2,1,0:T(8,128)S(1)}, u32[]{:S(2)}, u32[]{:S(2)}) %collective-permute-start.147) | collective-permute-done | bytes 9248 | tf_op jit(solution)/shard_map/ppermute | solution.py:653
  99.7 1.2 %shard_map.140 = (f32[27,32,128]{2,1,0:T(8,128)}, f32[32,32,128]{2,1,0:T(8,128)S(1)}, f32[2,9,128]{2,1,0:T(8,128)S(1)}, f32[2,9,128]{2,1,0:T(8,128)S(1)}, f32[3,...) custom-call(f32[32,32,128]{2,1,0:T(8,128)S(1)} %get-tuple-element.770.r_in, f32[32,32,128]{2,1,0:T(8,128)S(1)} %get-tuple-element.771.p_in, ...), custom_call_target="tpu_custom_call" | custom-call | flops 100000000 | bytes 10000000 | tf_op jit(solution)/shard_map/pallas_call | solution.py:545
  100.9 1.4 %collective-permute-start.152 = (f32[3,8,128]{2,1,0:T(8,128)S(1)}, f32[3,8,128]{2,1,0:T(8,128)S(1)}, u32[]{:S(2)}, u32[]{:S(2)}) collective-permute-start(f32[3,8,128]{2,1,0:T(8,128)S(1)} %get-tuple-element.780), channel_id=1, source_target_pairs={{0,1},{1,0},{2,3},{3,2},{4,5},{5,4},{6,7},{7,6},{8,9},{9,8},{10,11... | collective-permute-start | bytes 36872 | tf_op jit(solution)/shard_map/ppermute | solution.py:653
  102.3 0.5 collective-permute-start.150
  102.9 0.4 collective-permute-start.151
  103.2 0.5 collective-permute-done.150.h1
  103.7 3.3 %collective-permute-done.151.h2 = f32[2,9,128]{2,1,0:T(8,128)S(1)} collective-permute-done((f32[2,9,128]{2,1,0:T(8,128)S(1)}, f32[2,9,128]{2,1,0:T(8,128)S(1)}, u32[]{:S(2)}, u32[]{:S(2)}) %collective-permute-start.151) | collective-permute-done | bytes 9248 | tf_op jit(solution)/shard_map/ppermute | solution.py:653
  107.0 1.2 %to_coarsest.1 = f32[8,32,128]{2,1,0:T(8,128)} custom-call(f32[32,32,128]{2,1,0:T(8,128)S(1)} %get-tuple-element.777.r_in, f32[2,9,128]{2,1,0:T(8,128)S(1)} %collective-permute-done.150.h1, f32[2,9,128]{2,1,0:T(8,128)S(1)} %collective-permute-done.151.h2, f32[3,8,128]{2,1,0:T(8,128)S(1)} %collective-permute-done.152.g1, ...), custom_call_target="tpu_custom_call" | custom-call | flops 50000000 | bytes 1000000 | tf_op jit(solution)/shard_map/to_coarsest/pallas_call | solution.py:626
  (28 shorter events, 0.1 us)
Async XLA Ops:
  3.6 17.5 %collective-permute-start.128 = (f32[1,104,128]{2,1,0:T(8,128)S(1)}, f32[1,104,128]{2,1,0:T(8,128)S(1)}, u32[]{:S(2)}, u32[]{:S(2)}) collective-permute-start(f32[1,104,128]{2,1,0:T(8,128)S(1)} %get-tuple-element.735), channel_id=1, source_target_pairs={{0,4},{4,0},{8,12},{12,8},{16,20},{20,16},{24,28},{28,24},{1,5},{5... | collective-permute-start | bytes 159752 | tf_op jit(solution)/shard_map/ppermute | solution.py:653
  4.3 12.3 %collective-permute-start.13 = (f32[10,104,128]{2,1,0:T(8,128)S(1)}, f32[10,104,128]{2,1,0:T(8,128)S(1)}, u32[]{:S(2)}, u32[]{:S(2)}) collective-permute-start(f32[10,104,128]{2,1,0:T(8,128)S(1)} %get-tuple-element.361), channel_id=1, source_target_pairs={{0,0},{4,4},{8,8},{12,12},{16,16},{20,20},{24,24},{28,28},{1,1},{5... | collective-permute-start | bytes 1597448 | tf_op jit(solution)/shard_map/cond/branch_3_fun/ppermute | solution.py:644
  4.3 12.3 %collective-permute-start.14 = (f32[10,104,128]{2,1,0:T(8,128)S(1)}, f32[10,104,128]{2,1,0:T(8,128)S(1)}, u32[]{:S(2)}, u32[]{:S(2)}) collective-permute-start(f32[10,104,128]{2,1,0:T(8,128)S(1)} %get-tuple-element.362), channel_id=1, source_target_pairs={{0,0},{4,4},{8,8},{12,12},{16,16},{20,20},{24,24},{28,28},{1,1},{5... | collective-permute-start | bytes 1597448 | tf_op jit(solution)/shard_map/cond/branch_3_fun/ppermute | solution.py:644
  4.4 12.0 %collective-permute-start.12 = (f32[8,104,128]{2,1,0:T(8,128)S(1)}, f32[8,104,128]{2,1,0:T(8,128)S(1)}, u32[]{:S(2)}, u32[]{:S(2)}) collective-permute-start(f32[8,104,128]{2,1,0:T(8,128)S(1)} %get-tuple-element.360), channel_id=1, source_target_pairs={{0,4},{4,8},{8,12},{12,16},{16,20},{20,24},{24,28},{28,0},{1,5},{5... | collective-permute-start | bytes 1277960 | tf_op jit(solution)/shard_map/cond/branch_3_fun/ppermute | solution.py:644
  4.5 12.1 %collective-permute-start.15 = (f32[8,104,128]{2,1,0:T(8,128)S(1)}, f32[8,104,128]{2,1,0:T(8,128)S(1)}, u32[]{:S(2)}, u32[]{:S(2)}) collective-permute-start(f32[8,104,128]{2,1,0:T(8,128)S(1)} %get-tuple-element.363), channel_id=1, source_target_pairs={{0,28},{4,0},{8,4},{12,8},{16,12},{20,16},{24,20},{28,24},{1,29},{... | collective-permute-start | bytes 1277960 | tf_op jit(solution)/shard_map/cond/branch_3_fun/ppermute | solution.py:644
  18.2 4.7 %collective-permute-start.129 = (f32[1,104,128]{2,1,0:T(8,128)S(1)}, f32[1,104,128]{2,1,0:T(8,128)S(1)}, u32[]{:S(2)}, u32[]{:S(2)}) collective-permute-start(f32[1,104,128]{2,1,0:T(8,128)S(1)} %get-tuple-element.736), channel_id=1, source_target_pairs={{0,28},{4,8},{8,4},{12,16},{16,12},{20,24},{24,20},{28,0},{1,29},{... | collective-permute-start | bytes 159752 | tf_op jit(solution)/shard_map/ppermute | solution.py:653
  22.9 46.9 %copy-start = (f32[32,128,128]{2,1,0:T(8,128)S(1)}, f32[32,128,128]{2,1,0:T(8,128)}, u32[]{:S(2)}) copy-start(f32[32,128,128]{2,1,0:T(8,128)} %get-tuple-element.738.w_in) | copy-start | bytes 6291460
  22.9 46.9 %copy-start.1 = (f32[2,16,128]{2,1,0:T(8,128)S(1)}, f32[2,16,128]{2,1,0:T(8,128)}, u32[]{:S(2)}) copy-start(f32[2,16,128]{2,1,0:T(8,128)} %param.43) | copy-start | bytes 49156
  29.6 40.2 %collective-permute-start.130 = (f32[2,25,128]{2,1,0:T(8,128)S(1)}, f32[2,25,128]{2,1,0:T(8,128)S(1)}, u32[]{:S(2)}, u32[]{:S(2)}) collective-permute-start(f32[2,25,128]{2,1,0:T(8,128)S(1)} %get-tuple-element.744), channel_id=1, source_target_pairs={{0,4},{4,0},{8,12},{12,8},{16,20},{20,16},{24,28},{28,24},{1,5},{5... | collective-permute-start | bytes 76808 | tf_op jit(solution)/shard_map/ppermute | solution.py:653
  30.8 38.9 %collective-permute-start.131 = (f32[2,25,128]{2,1,0:T(8,128)S(1)}, f32[2,25,128]{2,1,0:T(8,128)S(1)}, u32[]{:S(2)}, u32[]{:S(2)}) collective-permute-start(f32[2,25,128]{2,1,0:T(8,128)S(1)} %get-tuple-element.745), channel_id=1, source_target_pairs={{0,28},{4,8},{8,4},{12,16},{16,12},{20,24},{24,20},{28,0},{1,29},{... | collective-permute-start | bytes 76808 | tf_op jit(solution)/shard_map/ppermute | solution.py:653
  32.3 37.4 %collective-permute-start.132 = (f32[5,8,128]{2,1,0:T(8,128)S(1)}, f32[5,8,128]{2,1,0:T(8,128)S(1)}, u32[]{:S(2)}, u32[]{:S(2)}) collective-permute-start(f32[5,8,128]{2,1,0:T(8,128)S(1)} %get-tuple-element.746), channel_id=1, source_target_pairs={{0,1},{1,0},{2,3},{3,2},{4,5},{5,4},{6,7},{7,6},{8,9},{9,8},{10,11... | collective-permute-start | bytes 61448 | tf_op jit(solution)/shard_map/ppermute | solution.py:653
  68.0 1.8 %collective-permute-start.133 = (f32[5,8,128]{2,1,0:T(8,128)S(1)}, f32[5,8,128]{2,1,0:T(8,128)S(1)}, u32[]{:S(2)}, u32[]{:S(2)}) collective-permute-start(f32[5,8,128]{2,1,0:T(8,128)S(1)} %get-tuple-element.747), channel_id=1, source_target_pairs={{0,4},{1,2},{2,1},{3,7},{4,0},{5,6},{6,5},{7,3},{8,12},{9,10},{10,... | collective-permute-start | bytes 61448 | tf_op jit(solution)/shard_map/ppermute | solution.py:664
  72.1 4.7 %collective-permute-start.134 = (f32[2,25,128]{2,1,0:T(8,128)S(1)}, f32[2,25,128]{2,1,0:T(8,128)S(1)}, u32[]{:S(2)}, u32[]{:S(2)}) collective-permute-start(f32[2,25,128]{2,1,0:T(8,128)S(1)} %get-tuple-element.750), channel_id=1, source_target_pairs={{0,4},{4,0},{8,12},{12,8},{16,20},{20,16},{24,28},{28,24},{1,5},{5... | collective-permute-start | bytes 76808 | tf_op jit(solution)/shard_map/ppermute | solution.py:653
  72.2 4.6 %collective-permute-start.135 = (f32[2,25,128]{2,1,0:T(8,128)S(1)}, f32[2,25,128]{2,1,0:T(8,128)S(1)}, u32[]{:S(2)}, u32[]{:S(2)}) collective-permute-start(f32[2,25,128]{2,1,0:T(8,128)S(1)} %get-tuple-element.751), channel_id=1, source_target_pairs={{0,28},{4,8},{8,4},{12,16},{16,12},{20,24},{24,20},{28,0},{1,29},{... | collective-permute-start | bytes 76808 | tf_op jit(solution)/shard_map/ppermute | solution.py:653
  72.8 3.9 %collective-permute-start.136 = (f32[5,8,128]{2,1,0:T(8,128)S(1)}, f32[5,8,128]{2,1,0:T(8,128)S(1)}, u32[]{:S(2)}, u32[]{:S(2)}) collective-permute-start(f32[5,8,128]{2,1,0:T(8,128)S(1)} %get-tuple-element.752), channel_id=1, source_target_pairs={{0,1},{1,0},{2,3},{3,2},{4,5},{5,4},{6,7},{7,6},{8,9},{9,8},{10,11... | collective-permute-start | bytes 61448 | tf_op jit(solution)/shard_map/ppermute | solution.py:653
  75.0 1.8 %collective-permute-start.137 = (f32[5,8,128]{2,1,0:T(8,128)S(1)}, f32[5,8,128]{2,1,0:T(8,128)S(1)}, u32[]{:S(2)}, u32[]{:S(2)}) collective-permute-start(f32[5,8,128]{2,1,0:T(8,128)S(1)} %get-tuple-element.753), channel_id=1, source_target_pairs={{0,4},{1,2},{2,1},{3,7},{4,0},{5,6},{6,5},{7,3},{8,12},{9,10},{10,... | collective-permute-start | bytes 61448 | tf_op jit(solution)/shard_map/ppermute | solution.py:664
  79.2 5.6 %collective-permute-start.138 = (f32[2,25,128]{2,1,0:T(8,128)S(1)}, f32[2,25,128]{2,1,0:T(8,128)S(1)}, u32[]{:S(2)}, u32[]{:S(2)}) collective-permute-start(f32[2,25,128]{2,1,0:T(8,128)S(1)} %get-tuple-element.756), channel_id=1, source_target_pairs={{0,4},{4,0},{8,12},{12,8},{16,20},{20,16},{24,28},{28,24},{1,5},{5... | collective-permute-start | bytes 76808 | tf_op jit(solution)/shard_map/ppermute | solution.py:653
  79.3 5.5 %collective-permute-start.139 = (f32[2,25,128]{2,1,0:T(8,128)S(1)}, f32[2,25,128]{2,1,0:T(8,128)S(1)}, u32[]{:S(2)}, u32[]{:S(2)}) collective-permute-start(f32[2,25,128]{2,1,0:T(8,128)S(1)} %get-tuple-element.757), channel_id=1, source_target_pairs={{0,28},{4,8},{8,4},{12,16},{16,12},{20,24},{24,20},{28,0},{1,29},{... | collective-permute-start | bytes 76808 | tf_op jit(solution)/shard_map/ppermute | solution.py:653
  81.1 3.8 %collective-permute-start.140 = (f32[5,8,128]{2,1,0:T(8,128)S(1)}, f32[5,8,128]{2,1,0:T(8,128)S(1)}, u32[]{:S(2)}, u32[]{:S(2)}) collective-permute-start(f32[5,8,128]{2,1,0:T(8,128)S(1)} %get-tuple-element.758), channel_id=1, source_target_pairs={{0,1},{1,0},{2,3},{3,2},{4,5},{5,4},{6,7},{7,6},{8,9},{9,8},{10,11... | collective-permute-start | bytes 61448 | tf_op jit(solution)/shard_map/ppermute | solution.py:653
  83.0 1.9 %collective-permute-start.141 = (f32[5,8,128]{2,1,0:T(8,128)S(1)}, f32[5,8,128]{2,1,0:T(8,128)S(1)}, u32[]{:S(2)}, u32[]{:S(2)}) collective-permute-start(f32[5,8,128]{2,1,0:T(8,128)S(1)} %get-tuple-element.759), channel_id=1, source_target_pairs={{0,4},{1,2},{2,1},{3,7},{4,0},{5,6},{6,5},{7,3},{8,12},{9,10},{10,... | collective-permute-start | bytes 61448 | tf_op jit(solution)/shard_map/ppermute | solution.py:664
  87.1 6.7 %collective-permute-start.144 = (f32[3,8,128]{2,1,0:T(8,128)S(1)}, f32[3,8,128]{2,1,0:T(8,128)S(1)}, u32[]{:S(2)}, u32[]{:S(2)}) collective-permute-start(f32[3,8,128]{2,1,0:T(8,128)S(1)} %get-tuple-element.768), channel_id=1, source_target_pairs={{0,1},{1,0},{2,3},{3,2},{4,5},{5,4},{6,7},{7,6},{8,9},{9,8},{10,11... | collective-permute-start | bytes 36872 | tf_op jit(solution)/shard_map/ppermute | solution.py:653
  89.1 4.6 %collective-permute-start.145 = (f32[3,8,128]{2,1,0:T(8,128)S(1)}, f32[3,8,128]{2,1,0:T(8,128)S(1)}, u32[]{:S(2)}, u32[]{:S(2)}) collective-permute-start(f32[3,8,128]{2,1,0:T(8,128)S(1)} %get-tuple-element.769), channel_id=1, source_target_pairs={{0,4},{1,2},{2,1},{3,7},{4,0},{5,6},{6,5},{7,3},{8,12},{9,10},{10,... | collective-permute-start | bytes 36872 | tf_op jit(solution)/shard_map/ppermute | solution.py:664
  89.1 1.3 %collective-permute-start.142 = (f32[2,9,128]{2,1,0:T(8,128)S(1)}, f32[2,9,128]{2,1,0:T(8,128)S(1)}, u32[]{:S(2)}, u32[]{:S(2)}) collective-permute-start(f32[2,9,128]{2,1,0:T(8,128)S(1)} %get-tuple-element.766), channel_id=1, source_target_pairs={{0,4},{4,0},{8,12},{12,8},{16,20},{20,16},{24,28},{28,24},{1,5},{5... | collective-permute-start | bytes 27656 | tf_op jit(solution)/shard_map/ppermute | solution.py:653
  89.6 4.1 %collective-permute-start.143 = (f32[2,9,128]{2,1,0:T(8,128)S(1)}, f32[2,9,128]{2,1,0:T(8,128)S(1)}, u32[]{:S(2)}, u32[]{:S(2)}) collective-permute-start(f32[2,9,128]{2,1,0:T(8,128)S(1)} %get-tuple-element.767), channel_id=1, source_target_pairs={{0,28},{4,8},{8,4},{12,16},{16,12},{20,24},{24,20},{28,0},{1,29},{... | collective-permute-start | bytes 27656 | tf_op jit(solution)/shard_map/ppermute | solution.py:653
  94.9 4.8 %collective-permute-start.148 = (f32[3,8,128]{2,1,0:T(8,128)S(1)}, f32[3,8,128]{2,1,0:T(8,128)S(1)}, u32[]{:S(2)}, u32[]{:S(2)}) collective-permute-start(f32[3,8,128]{2,1,0:T(8,128)S(1)} %get-tuple-element.774), channel_id=1, source_target_pairs={{0,1},{1,0},{2,3},{3,2},{4,5},{5,4},{6,7},{7,6},{8,9},{9,8},{10,11... | collective-permute-start | bytes 36872 | tf_op jit(solution)/shard_map/ppermute | solution.py:653
  95.0 4.7 %collective-permute-start.149 = (f32[3,8,128]{2,1,0:T(8,128)S(1)}, f32[3,8,128]{2,1,0:T(8,128)S(1)}, u32[]{:S(2)}, u32[]{:S(2)}) collective-permute-start(f32[3,8,128]{2,1,0:T(8,128)S(1)} %get-tuple-element.775), channel_id=1, source_target_pairs={{0,4},{1,2},{2,1},{3,7},{4,0},{5,6},{6,5},{7,3},{8,12},{9,10},{10,... | collective-permute-start | bytes 36872 | tf_op jit(solution)/shard_map/ppermute | solution.py:664
  95.0 1.3 %collective-permute-start.146 = (f32[2,9,128]{2,1,0:T(8,128)S(1)}, f32[2,9,128]{2,1,0:T(8,128)S(1)}, u32[]{:S(2)}, u32[]{:S(2)}) collective-permute-start(f32[2,9,128]{2,1,0:T(8,128)S(1)} %get-tuple-element.772), channel_id=1, source_target_pairs={{0,4},{4,0},{8,12},{12,8},{16,20},{20,16},{24,28},{28,24},{1,5},{5... | collective-permute-start | bytes 27656 | tf_op jit(solution)/shard_map/ppermute | solution.py:653
  95.5 4.1 %collective-permute-start.147 = (f32[2,9,128]{2,1,0:T(8,128)S(1)}, f32[2,9,128]{2,1,0:T(8,128)S(1)}, u32[]{:S(2)}, u32[]{:S(2)}) collective-permute-start(f32[2,9,128]{2,1,0:T(8,128)S(1)} %get-tuple-element.773), channel_id=1, source_target_pairs={{0,28},{4,8},{8,4},{12,16},{16,12},{20,24},{24,20},{28,0},{1,29},{... | collective-permute-start | bytes 27656 | tf_op jit(solution)/shard_map/ppermute | solution.py:653
  100.9 6.0 %collective-permute-start.152 = (f32[3,8,128]{2,1,0:T(8,128)S(1)}, f32[3,8,128]{2,1,0:T(8,128)S(1)}, u32[]{:S(2)}, u32[]{:S(2)}) collective-permute-start(f32[3,8,128]{2,1,0:T(8,128)S(1)} %get-tuple-element.780), channel_id=1, source_target_pairs={{0,1},{1,0},{2,3},{3,2},{4,5},{5,4},{6,7},{7,6},{8,9},{9,8},{10,11... | collective-permute-start | bytes 36872 | tf_op jit(solution)/shard_map/ppermute | solution.py:653
  102.3 4.6 %collective-permute-start.153 = (f32[3,8,128]{2,1,0:T(8,128)S(1)}, f32[3,8,128]{2,1,0:T(8,128)S(1)}, u32[]{:S(2)}, u32[]{:S(2)}) collective-permute-start(f32[3,8,128]{2,1,0:T(8,128)S(1)} %get-tuple-element.781), channel_id=1, source_target_pairs={{0,4},{1,2},{2,1},{3,7},{4,0},{5,6},{6,5},{7,3},{8,12},{9,10},{10,... | collective-permute-start | bytes 36872 | tf_op jit(solution)/shard_map/ppermute | solution.py:664
  102.3 1.3 %collective-permute-start.150 = (f32[2,9,128]{2,1,0:T(8,128)S(1)}, f32[2,9,128]{2,1,0:T(8,128)S(1)}, u32[]{:S(2)}, u32[]{:S(2)}) collective-permute-start(f32[2,9,128]{2,1,0:T(8,128)S(1)} %get-tuple-element.778), channel_id=1, source_target_pairs={{0,4},{4,0},{8,12},{12,8},{16,20},{20,16},{24,28},{28,24},{1,5},{5... | collective-permute-start | bytes 27656 | tf_op jit(solution)/shard_map/ppermute | solution.py:653
  102.9 4.1 %collective-permute-start.151 = (f32[2,9,128]{2,1,0:T(8,128)S(1)}, f32[2,9,128]{2,1,0:T(8,128)S(1)}, u32[]{:S(2)}, u32[]{:S(2)}) collective-permute-start(f32[2,9,128]{2,1,0:T(8,128)S(1)} %get-tuple-element.779), channel_id=1, source_target_pairs={{0,28},{4,8},{8,4},{12,16},{16,12},{20,24},{24,20},{28,0},{1,29},{... | collective-permute-start | bytes 27656 | tf_op jit(solution)/shard_map/ppermute | solution.py:653
